TPU v7x, 128 devices: a whole 4x4x4 slice. The times are simulated.
128 devices in a mesh: dep: 4 (over z), col: 4 (over y), row: 8 (over x, core).
Axes of the slice: x: 4, y: 4, z: 4, core: 2. Of those that a mesh axis runs over, the one named last changes fastest.
Arguments:
- x_tok: bfloat16 [8192, 4096], P(('dep', 'row'), 'col')
- w_up: bfloat16 [4096, 16384], P('row', 'col')
- w_down: bfloat16 [16384, 4096], P('row', 'col')
- grad_out: bfloat16 [8192, 4096], P(('dep', 'row'), 'col')
Outputs:
- output 1: bfloat16 [8192, 4096], P(('dep', 'row'), 'col')
- output 2: bfloat16 [8192, 4096], P(('dep', 'row'), 'col')
- output 3: float32 [4096, 16384], P(('row', 'dep'), 'col')
- output 4: float32 [16384, 4096], P(('row', 'dep'), 'col')
All inputs are finite; a program needn't handle non-finite values.
Results may differ from a plain program's by a relative error of at most 0.001.
Values are sent between devices in bfloat16 or wider.
A program may use at most 1 GiB of HBM per device.

v0:
```python
import jax
import jax.numpy as jnp
from jax import lax
from jax.sharding import PartitionSpec as P, NamedSharding

GELU_COEF = 0.7978845608028654
CUBIC_COEF = 0.044715


def gelu_fwd(pre_act):
    inner = GELU_COEF * (pre_act + CUBIC_COEF * pre_act * pre_act * pre_act)
    return 0.5 * pre_act * (1.0 + jnp.tanh(inner))


def gelu_slope(pre_act):
    inner = GELU_COEF * (pre_act + CUBIC_COEF * pre_act * pre_act * pre_act)
    tanh_val = jnp.tanh(inner)
    return 0.5 * (1.0 + tanh_val) + 0.5 * pre_act * (1.0 - tanh_val * tanh_val) * GELU_COEF * (1.0 + 3.0 * CUBIC_COEF * pre_act * pre_act)


def solution(mesh):
    act_spec = P(("dep", "row"), "col")
    wgt_spec = P("row", "col")
    grad_spec = P(("row", "dep"), "col")

    def local_block(x_loc, w_up_loc, w_down_loc, g_loc):
        x_full = lax.all_gather(x_loc, "col", axis=1, tiled=True)
        w_up_cols = lax.all_gather(w_up_loc, "row", axis=0, tiled=True)
        pre_act = jnp.dot(x_full, w_up_cols, preferred_element_type=jnp.float32)
        hidden_act = gelu_fwd(pre_act).astype(jnp.bfloat16)
        act_full = lax.all_gather(hidden_act, "col", axis=1, tiled=True)
        w_down_cols = lax.all_gather(w_down_loc, "row", axis=0, tiled=True)
        y_loc = jnp.dot(act_full, w_down_cols, preferred_element_type=jnp.float32).astype(jnp.bfloat16)
        d_act_part = jnp.einsum("th,fh->tf", g_loc, w_down_cols, preferred_element_type=jnp.float32)
        d_act = lax.psum_scatter(d_act_part, "col", scatter_dimension=1, tiled=True)
        d_pre = (d_act * gelu_slope(pre_act)).astype(jnp.bfloat16)
        dx_part = jnp.einsum("tf,hf->th", d_pre, w_up_cols, preferred_element_type=jnp.float32)
        dx_loc = lax.psum_scatter(dx_part, "col", scatter_dimension=1, tiled=True).astype(jnp.bfloat16)
        x_layer = lax.all_to_all(x_full, "row", 1, 0, tiled=True)
        d_pre_layer = lax.all_gather(d_pre, "row", axis=0, tiled=True)
        dw_up_part = jnp.einsum("th,tf->hf", x_layer, d_pre_layer, preferred_element_type=jnp.float32)
        dw_up_loc = lax.psum_scatter(dw_up_part, "dep", scatter_dimension=0, tiled=True)
        act_layer = lax.all_to_all(act_full, "row", 1, 0, tiled=True)
        g_layer = lax.all_gather(g_loc, "row", axis=0, tiled=True)
        dw_down_part = jnp.einsum("tf,th->fh", act_layer, g_layer, preferred_element_type=jnp.float32)
        dw_down_loc = lax.psum_scatter(dw_down_part, "dep", scatter_dimension=0, tiled=True)
        return y_loc, dx_loc, dw_up_loc, dw_down_loc

    return jax.shard_map(local_block, mesh=mesh, in_specs=(act_spec, wgt_spec, wgt_spec, act_spec), out_specs=(act_spec, act_spec, grad_spec, grad_spec), check_vma=False)
```

profile of v0, /device:TPU:1, one launch (start us, length us, event | category | flops | bytes accessed | tf_op | source)
XLA Modules:
  0.0 1010.1 jit_solution(5745499602142145404)
XLA Ops:
  8.2 1.0 copy.11
  10.0 160.0 %all-gather.13.cloned.1.call-done = bf16[16384,1024]{1,0:T(8,128)(2,1)} async-done(((bf16[2048,1024]{1,0:T(8,128)(2,1)}), bf16[16384,1024]{1,0:T(8,128)(2,1)}) %all-gather.13.cloned.1.call-update) | async-done | bytes 33554448 | tf_op jit(solution)/shard_map/all_gather | solution.py:32
  170.1 21.1 %fusion.7 = f32[256,16384]{1,0:T(8,128)} fusion(bf16[256,1024]{1,0:T(8,128)(2,1)S(1)} %copy-done.2, bf16[16384,1024]{1,0:T(8,128)(2,1)} %all-gather.13.cloned.1.call-done), kind=kOutput, calls=%fused_computation.13 | convolution fusion | flops 8589934592 | bytes 50855936 | tf_op jit(solution)/shard_map/th,fh->tf/dot_general | solution.py:34
  191.2 11.9 %all-gather.7.cloned.1.call-done = bf16[256,4096]{0,1:T(8,128)(2,1)} async-done(((bf16[256,1024]{0,1:T(8,128)(2,1)}), bf16[256,4096]{0,1:T(8,128)(2,1)}) %all-gather.7.cloned.1.call-update) | async-done | bytes 2097168 | tf_op jit(solution)/shard_map/all_gather | solution.py:27
  203.2 159.1 %all-gather.9.cloned.1.call-done = bf16[4096,4096]{1,0:T(8,128)(2,1)} async-done(((bf16[512,4096]{1,0:T(8,128)(2,1)}), bf16[4096,4096]{1,0:T(8,128)(2,1)}) %all-gather.9.cloned.1.call-update) | async-done | bytes 33554448 | tf_op jit(solution)/shard_map/all_gather | solution.py:28
  362.3 150.6 %reduce-scatter.5.cloned.1.call-done = f32[256,4096]{1,0:T(8,128)} async-done(((f32[256,16384]{1,0:T(8,128)}), f32[256,4096]{1,0:T(8,128)}) %reduce-scatter.5.cloned.1.call-update) | async-done | bytes 4194320 | tf_op jit(solution)/shard_map/reduce_scatter | solution.py:35
  512.9 19.8 %fusion.6 = (bf16[256,4096]{1,0:T(8,128)(2,1)}, bf16[256,4096]{1,0:T(8,128)(2,1)}) fusion(f32[256,4096]{1,0:T(8,128)} %reduce-scatter.5.cloned.1.call-done, bf16[256,4096]{0,1:T(8,128)(2,1)} %all-gather.7.cloned.1.call-done, bf16[4096,4096]{1,0:T(8,128)(2,1)} %all-gather.9.cloned.1.call-done), kind=kOutput, calls=%fused_computation.10 | convolution fusion | flops 8611954688 | bytes 44040192 | tf_op jit(solution)/shard_map/dot_general | solution.py:29
  533.3 0.7 all-gather.17.cloned.1.call-update
  534.3 16.1 %fusion.8 = f32[256,4096]{1,0:T(8,128)} fusion(bf16[256,4096]{1,0:T(8,128)(2,1)S(1)} %copy-done, bf16[4096,4096]{1,0:T(8,128)(2,1)} %all-gather.9.cloned.1.call-done), kind=kOutput, calls=%fused_computation.14 | convolution fusion | flops 8589934592 | bytes 39845888 | tf_op jit(solution)/shard_map/tf,hf->th/dot_general | solution.py:37
  550.5 54.1 %all_to_all.38 = bf16[256,8,512]{0,2,1:T(8,128)(2,1)S(1)} all-to-all(bf16[256,8,512]{0,2,1:T(8,128)(2,1)} %bitcast.27), channel_id=1, replica_groups=mesh['dep'=4,'col'=4,'row'=8] {'row'}, dimensions={1} | all-to-all | bytes 4194304 | tf_op jit(solution)/shard_map/all_to_all | solution.py:39
  604.5 2.4 copy.12
  606.9 33.9 %all-gather.15.cloned.1.call-done = bf16[2048,4096]{1,0:T(8,128)(2,1)} async-done(((bf16[256,4096]{1,0:T(8,128)(2,1)}), bf16[2048,4096]{1,0:T(8,128)(2,1)}) %all-gather.15.cloned.1.call-update) | async-done | bytes 16777232 | tf_op jit(solution)/shard_map/all_gather | solution.py:40
  640.8 15.1 %convolution_bitcast_fusion = f32[512,4096]{0,1:T(8,128)} fusion(bf16[2048,4096]{1,0:T(8,128)(2,1)} %all-gather.15.cloned.1.call-done, bf16[2048,512]{1,0:T(8,128)(2,1)} %bitcast.28), kind=kOutput, calls=%fused_computation.1 | convolution fusion | flops 8589934592 | bytes 27262976 | tf_op jit(solution)/shard_map/th,tf->hf/dot_general | solution.py:41
  655.9 70.2 %all-gather.11.cloned.1.call-done = bf16[256,16384]{1,0:T(8,128)(2,1)} async-done(((bf16[256,4096]{1,0:T(8,128)(2,1)}), bf16[256,16384]{1,0:T(8,128)(2,1)}) %all-gather.11.cloned.1.call-update) | async-done | bytes 8388624 | tf_op jit(solution)/shard_map/all_gather | solution.py:31
  726.2 8.3 copy.17
  734.5 5.8 all-to-all-start.1
  740.2 48.2 %all-gather.17.cloned.1.call-done = bf16[2048,1024]{1,0:T(8,128)(2,1)} async-done(((bf16[256,1024]{1,0:T(8,128)(2,1)}), bf16[2048,1024]{1,0:T(8,128)(2,1)}) %all-gather.17.cloned.1.call-update) | async-done | bytes 4194320 | tf_op jit(solution)/shard_map/all_gather | solution.py:44
  788.4 61.3 %all-to-all-done.1 = bf16[256,8,2048]{2,0,1:T(8,128)(2,1)} async-done(((bf16[256,8,2048]{2,0,1:T(8,128)(2,1)}), bf16[256,8,2048]{2,0,1:T(8,128)(2,1)}, u32[]{:S(2)}, u32[]{:S(2)}) %all-to-all-start.1) | async-done | bytes 8388640 | tf_op jit(solution)/shard_map/all_to_all | solution.py:43
  849.7 14.6 %fusion.9 = f32[2048,1024]{1,0:T(8,128)} fusion(bf16[2048,2048]{1,0:T(8,128)(2,1)} %bitcast.5, bf16[2048,1024]{1,0:T(8,128)(2,1)} %all-gather.17.cloned.1.call-done), kind=kOutput, calls=%fused_computation.15 | convolution fusion | flops 8589934592 | bytes 20971520 | tf_op jit(solution)/shard_map/tf,th->fh/dot_general | solution.py:45
  864.4 2.1 convert_element_type.15
  866.5 18.2 %convolution_convert_fusion = bf16[256,1024]{1,0:T(8,128)(2,1)} fusion(bf16[256,16384]{1,0:T(8,128)(2,1)} %all-gather.11.cloned.1.call-done, bf16[16384,1024]{1,0:T(8,128)(2,1)} %all-gather.13.cloned.1.call-done), kind=kOutput, calls=%fused_computation.12 | convolution fusion | flops 8590196736 | bytes 42467328 | tf_op jit(solution)/shard_map/dot_general | solution.py:33
  884.7 35.3 %reduce-scatter.9.cloned.1.call-done = f32[128,4096]{0,1:T(8,128)} async-done(((f32[512,4096]{0,1:T(8,128)}), f32[128,4096]{0,1:T(8,128)}) %reduce-scatter.9.cloned.1.call-update) | async-done | bytes 2097168 | tf_op jit(solution)/shard_map/reduce_scatter | solution.py:42
  920.0 2.9 copy.14
  922.9 80.4 %reduce-scatter.11.cloned.1.call-done = f32[512,1024]{1,0:T(8,128)} async-done(((f32[2048,1024]{1,0:T(8,128)}), f32[512,1024]{1,0:T(8,128)}) %reduce-scatter.11.cloned.1.call-update) | async-done | bytes 2097168 | tf_op jit(solution)/shard_map/reduce_scatter | solution.py:46
  (26 shorter events, 2.8 us)
Async XLA Ops:
  7.2 1.0 copy-start.1
  7.2 162.9 %all-gather.13.cloned.1.call-start = ((), (), s32[]{:S(2)}) async-start(), calls=%async_computation.9 | async-start | bytes 37748736 | tf_op jit(solution)/shard_map/all_gather | solution.py:32
  7.2 162.8 %copy-start.2 = (bf16[256,1024]{1,0:T(8,128)(2,1)S(1)}, bf16[256,1024]{1,0:T(8,128)(2,1)}, u32[]{:S(2)}) copy-start(bf16[256,1024]{1,0:T(8,128)(2,1)} %param.7) | copy-start | bytes 1572868
  7.9 195.3 %all-gather.7.cloned.1.call-start = ((), (), s32[]{:S(2)}) async-start(), calls=%async_computation.6 | async-start | bytes 2621440 | tf_op jit(solution)/shard_map/all_gather | solution.py:27
  9.2 353.0 %all-gather.9.cloned.1.call-start = ((), (), s32[]{:S(2)}) async-start(), calls=%async_computation.7 | async-start | bytes 37748736 | tf_op jit(solution)/shard_map/all_gather | solution.py:28
  10.0 502.9 %reduce-scatter.5.cloned.1.call-start = ((), (), s32[]{:S(2)}) async-start(), calls=%async_computation.10 | async-start | bytes 20971520 | tf_op jit(solution)/shard_map/reduce_scatter | solution.py:35
  191.2 449.6 %all-gather.15.cloned.1.call-start = ((), (), s32[]{:S(2)}) async-start(), calls=%async_computation.12 | async-start | bytes 18874368 | tf_op jit(solution)/shard_map/all_gather | solution.py:40
  532.7 1.6 copy-start
  532.7 193.5 %all-gather.11.cloned.1.call-start = ((), (), s32[]{:S(2)}) async-start(), calls=%async_computation.8 | async-start | bytes 10485760 | tf_op jit(solution)/shard_map/all_gather | solution.py:31
  533.3 255.2 %all-gather.17.cloned.1.call-start = ((), (), s32[]{:S(2)}) async-start(), calls=%async_computation.14 | async-start | bytes 4718592 | tf_op jit(solution)/shard_map/all_gather | solution.py:44
  534.0 330.3 %reduce-scatter.7.cloned.1.call-start = ((), (), s32[]{:S(2)}) async-start(), calls=%async_computation.11 | async-start | bytes 5242880 | tf_op jit(solution)/shard_map/reduce_scatter | solution.py:38
  550.4 369.6 %reduce-scatter.9.cloned.1.call-start = ((), (), s32[]{:S(2)}) async-start(), calls=%async_computation.13 | async-start | bytes 10485760 | tf_op jit(solution)/shard_map/reduce_scatter | solution.py:42
  734.5 115.3 %all-to-all-start.1 = ((bf16[256,8,2048]{2,0,1:T(8,128)(2,1)}), bf16[256,8,2048]{2,0,1:T(8,128)(2,1)}, u32[]{:S(2)}, u32[]{:S(2)}) async-start(bf16[256,8,2048]{2,0,1:T(8,128)(2,1)} %bitcast.24), calls=%async_computation.4 | async-start | bytes 16777216 | tf_op jit(solution)/shard_map/all_to_all | solution.py:43
  740.2 263.0 %reduce-scatter.11.cloned.1.call-start = ((), (), s32[]{:S(2)}) async-start(), calls=%async_computation.15 | async-start | bytes 10485760 | tf_op jit(solution)/shard_map/reduce_scatter | solution.py:46
Sparse Core Ops, SparseCore 0:
  9.7 160.3 all-gather.12
  172.3 30.8 all-gather.6
  204.9 157.3 all-gather.8
  364.6 148.2 reduce-scatter.4
  532.8 107.9 all-gather.14
  642.9 83.2 all-gather.10
  727.9 60.4 all-gather.16
  790.8 46.1 reduce-scatter.6
  839.5 80.4 reduce-scatter.8
  922.9 80.3 reduce-scatter.10
where the time goes:
time: 1010 us
  waiting for transfers between devices  814 us (81%)
  matrix products  105 us (10%)
  blocking collectives  54.1 us (5%)
  local copies, waits for them, and re-layouts  15 us (1%)
  between operations  14.2 us (1%)
    all_gather x1, waiting for transfers between devices, local_block(): w_down_cols = lax.all_gather(w_down_loc, 'row', axis=0, tiled=True)  160 us
    all_gather x1, waiting for transfers between devices, local_block(): w_up_cols = lax.all_gather(w_up_loc, 'row', axis=0, tiled=True)  159 us
    reduce_scatter x1, waiting for transfers between devices, local_block(): d_act = lax.psum_scatter(d_act_part, 'col', scatter_dimension=1, tiled=True)  151 us
    reduce_scatter x1, waiting for transfers between devices, local_block(): lax.psum_scatter(dw_down_part, 'dep', scatter_dimension=0, tiled=True)  80.4 us
    all_gather x1, waiting for transfers between devices, local_block(): act_full = lax.all_gather(hidden_act, 'col', axis=1, tiled=True)  70.2 us
    all_to_all x1, waiting for transfers between devices, local_block(): act_layer = lax.all_to_all(act_full, 'row', 1, 0, tiled=True)  61.3 us
    all_to_all x1, blocking collectives, local_block(): x_layer = lax.all_to_all(x_full, 'row', 1, 0, tiled=True)  54.1 us
    all_gather x1, waiting for transfers between devices, local_block(): g_layer = lax.all_gather(g_loc, 'row', axis=0, tiled=True)  48.2 us
  transfers between devices with their start and end apart: 11, of which 10 were waited for; matrix products, arithmetic and copies ran while one was open for 10% of the time, Pallas kernels for 0%

commit v1 on v0

v1 whole, which is shorter than its diff:
```python
import jax
import jax.numpy as jnp
from jax import lax
from jax.experimental import pallas as pl
from jax.experimental.pallas import tpu as pltpu
from jax.sharding import PartitionSpec as P

GELU_COEF = 0.7978845608028654
CUBIC_COEF = 0.044715
NX = 4
NY = 4
NZ = 4


def gelu_fwd(pre_act):
    inner = GELU_COEF * (pre_act + CUBIC_COEF * pre_act * pre_act * pre_act)
    return 0.5 * pre_act * (1.0 + jnp.tanh(inner))


def gelu_slope(pre_act):
    inner = GELU_COEF * (pre_act + CUBIC_COEF * pre_act * pre_act * pre_act)
    tanh_val = jnp.tanh(inner)
    return 0.5 * (1.0 + tanh_val) + 0.5 * pre_act * (1.0 - tanh_val * tanh_val) * GELU_COEF * (1.0 + 3.0 * CUBIC_COEF * pre_act * pre_act)


def rot(v, d, n):
    return lax.rem(v + (d % n), n)


class Net:
    def __init__(self, send_sem, recv_sem):
        self.send_sem, self.recv_sem = send_sem, recv_sem
        self.used = 0
        self.sent = []
        self.z = lax.axis_index("dep")
        self.y = lax.axis_index("col")
        row = lax.axis_index("row")
        self.row = row
        self.x = lax.div(row, 2)
        self.k = lax.rem(row, 2)

    def slots(self, n):
        base = self.used
        self.used += n
        return base

    def make(self, src, dst, where, send_slot, recv_slot):
        return pltpu.make_async_remote_copy(
            src_ref=src, dst_ref=dst, send_sem=self.send_sem.at[send_slot], recv_sem=self.recv_sem.at[recv_slot],
            device_id=where, device_id_type=pl.DeviceIdType.MESH)

    def send(self, src, dst, where):
        slot = self.slots(1)
        copy = self.make(src, dst, where, slot, slot)
        copy.start()
        self.sent.append(copy)
        return copy

    def finish(self):
        for copy in self.sent:
            copy.wait_send()

    def at_x(self, d):
        return {"row": 2 * rot(self.x, d, NX) + self.k}

    def at_y(self, d):
        return {"col": rot(self.y, d, NY)}

    def at_z(self, d):
        return {"dep": rot(self.z, d, NZ)}

    def partner(self):
        return {"row": 2 * self.x + 1 - self.k}


def ring(net, place, n, up, down, own, view, arrived):
    e_lo = net.send(own(0), view(place, 0), up)
    w_hi = net.send(own(1), view(place, 1), down)
    e_hi = net.send(own(1), view(place, 1), up)
    w_lo = net.send(own(0), view(place, 0), down)
    west, east, far = rot(place, -1, n), rot(place, 1, n), rot(place, 2, n)
    yield
    e_lo.wait_recv()
    on_up = net.send(view(west, 0), view(west, 0), up)
    arrived(west, 0)
    yield
    w_hi.wait_recv()
    on_down = net.send(view(east, 1), view(east, 1), down)
    arrived(east, 1)
    yield
    e_hi.wait_recv()
    arrived(west, 1)
    w_lo.wait_recv()
    arrived(east, 0)
    yield
    on_up.wait_recv()
    arrived(far, 0)
    on_down.wait_recv()
    arrived(far, 1)


def to_z(net, view, got):
    def arrived(i, half):
        got.append(net.send(view(i, half), view(i, half), net.at_z(1 if half == 0 else -1)))
    return arrived


def gather_w1(net, w1, w1f, buf, sem):
    rows, cols = w1.shape[0], w1f.shape[1]
    half = rows // 2
    parity = lax.rem(net.z, 2)
    mine = pl.ds(pl.multiple_of(net.k * cols, cols), cols)
    other = pl.ds(pl.multiple_of((1 - net.k) * cols, cols), cols)
    own_rows = pl.ds(pl.multiple_of(net.row * rows, rows), rows)
    load = pltpu.make_async_copy(w1.at[:, mine], buf, sem.at[0])
    load.start()
    swap = net.send(w1.at[:, other], w1f.at[own_rows, :], net.partner())
    load.wait()
    store = pltpu.make_async_copy(buf, w1f.at[own_rows, :], sem.at[0])
    store.start()
    yield
    swap.wait_recv()
    store.wait()

    def view(i, h):
        return w1f.at[pl.ds(pl.multiple_of((2 * i + parity) * rows + h * half, half), half), :]

    got = []
    yield from ring(net, net.x, NX, net.at_x(1), net.at_x(-1), lambda h: view(net.x, h), view, to_z(net, view, got))
    yield
    for copy in got:
        copy.wait_recv()


def gather_tokens(net, src, dst, buf, sem):
    rows, cols = src.shape
    rs = pl.ds(pl.multiple_of(net.k * rows, rows), rows)

    def view(j):
        return dst.at[rs, pl.ds(pl.multiple_of(j * cols, cols), cols)]

    load = pltpu.make_async_copy(src, buf, sem)
    load.start()
    copies = [net.send(src, view(net.y), net.at_y(d)) for d in (1, 3, 2)]
    passed = [net.send(src, view(net.y), net.partner())]
    load.wait()
    store = pltpu.make_async_copy(buf, view(net.y), sem)
    store.start()
    yield
    for d, copy in zip((1, 3, 2), copies):
        copy.wait_recv()
        piece = view(rot(net.y, -d, NY))
        passed.append(net.send(piece, piece, net.partner()))
        yield
    store.wait()
    for copy in passed:
        copy.wait_recv()


def scatter(net, pieces, slot_of, dev_of, self_piece, is_self, here, arrivals, sender, buf, sem):
    send_base, recv_base = net.slots(4), 0
    load = pltpu.make_async_copy(self_piece, buf, sem)
    load.start()
    copies = []
    for s in range(4):
        copy = net.make(pieces(s), slot_of(s), dev_of(s), send_base + s, send_base + sender)
        stays = is_self(s)
        copies.append((copy, stays))

        @pl.when(jnp.logical_not(stays))
        def _():
            copy.start()

    load.wait()

    @pl.when(here)
    def _():
        pltpu.make_async_copy(buf, arrivals(sender), net.recv_sem.at[send_base + sender]).start()

    yield
    for i in range(4):
        net.make(buf, arrivals(i), dev_of(0), send_base, send_base + i).wait_recv()
    yield
    for copy, stays in copies:
        @pl.when(jnp.logical_not(stays))
        def _():
            copy.wait_send()


def scatter_w2(net, w2, w2s, buf, sem):
    rows, cols = w2.shape
    part = rows // 8
    parity = lax.rem(net.z, 2)

    def piece(s):
        return w2.at[pl.ds(pl.multiple_of(parity * 4 * part + s * part, part), part), :]

    def slot(j):
        return w2s.at[:, pl.ds(pl.multiple_of(j * cols, cols), cols)]

    yield from scatter(
        net, piece, lambda s: slot(net.y), lambda s: {"col": net.x, "row": 2 * s + net.k}, piece(net.x),
        lambda s: jnp.logical_and(net.x == s, net.y == net.x), net.x == net.y, slot, net.y, buf, sem)


def gather_w2(net, w2s, w2f, buf, sem):
    rows = w2s.shape[0]
    half = rows // 2
    parity = lax.rem(net.z, 2)
    load = pltpu.make_async_copy(w2s, buf, sem)
    load.start()

    def view(i, h):
        return w2f.at[pl.ds(pl.multiple_of(parity * 4 * rows + i * rows + h * half, half), half), :]

    got = []
    arrived = to_z(net, view, got)
    gather = ring(net, net.x, NX, net.at_x(1), net.at_x(-1), lambda h: w2s.at[pl.ds(h * half, half), :], view, arrived)
    next(gather)
    got.append(net.send(w2s.at[pl.ds(0, half), :], view(net.x, 0), net.at_z(1)))
    got.append(net.send(w2s.at[pl.ds(half, half), :], view(net.x, 1), net.at_z(-1)))
    load.wait()
    store = pltpu.make_async_copy(buf, w2f.at[pl.ds(pl.multiple_of(parity * 4 * rows + net.x * rows, rows), rows), :], sem)
    store.start()
    yield
    yield from gather
    yield
    for copy in got:
        copy.wait_recv()
    store.wait()


def move_act(net, act, act_l, buf, sem):
    part = act_l.shape[2]
    yield from scatter(
        net, lambda s: act.at[pl.ds(s * part, part), :], lambda s: act_l.at[net.x, s],
        lambda s: {"row": 2 * net.y + net.k, "col": s}, act.at[pl.ds(pl.multiple_of(net.y * part, part), part), :],
        lambda s: jnp.logical_and(net.y == s, net.x == net.y), net.x == net.y,
        lambda i: act_l.at[i, net.y], net.x, buf, sem)

    def view(j, h):
        return act_l.at[pl.ds(2 * h, 2), j]

    yield from ring(net, net.y, NY, net.at_y(1), net.at_y(-1), lambda h: view(net.y, h), view, lambda i, h: None)


def layer_tokens(net, own, piece, dst, buf, sem):
    load = pltpu.make_async_copy(own, buf, sem)
    load.start()
    copies = [net.send(piece(d), dst.at[net.row], net.at_x(d)) for d in (1, 3, 2)]
    passed = [net.send(own, dst.at[net.row], net.partner())]
    load.wait()
    store = pltpu.make_async_copy(buf, dst.at[net.row], sem)
    store.start()
    yield
    for d, copy in zip((1, 3, 2), copies):
        copy.wait_recv()
        block = dst.at[2 * rot(net.x, -d, NX) + net.k]
        passed.append(net.send(block, block, net.partner()))
        yield
    store.wait()
    for copy in passed:
        copy.wait_recv()


def gather_dpre(net, d_pre, d_pre_l, buf, sem):
    half = d_pre.shape[0] // 2
    load = pltpu.make_async_copy(d_pre, buf, sem)
    load.start()

    def view(i, h):
        return d_pre_l.at[i, pl.ds(h * half, half), :]

    gather = ring(net, net.x, NX, net.at_x(1), net.at_x(-1), lambda h: d_pre.at[pl.ds(h * half, half), :], view, lambda i, h: None)
    next(gather)
    load.wait()
    store = pltpu.make_async_copy(buf, d_pre_l.at[net.x], sem)
    store.start()
    yield
    yield from gather
    store.wait()


def exchange_sums(net, part, dst):
    cols = dst.shape[2]
    copies = []
    for d in (1, 3, 2):
        src = part.at[:, pl.ds(pl.multiple_of(rot(net.y, d, NY) * cols, cols), cols)]
        copies.append(net.send(src, dst.at[d - 1], net.at_y(d)))
    yield
    for copy in copies:
        copy.wait_recv()


def run(flows):
    flows = list(flows)
    while flows:
        flows = [f for f in flows if next(f, flows) is not flows]


def first_gather(w1, w2, x, g, w1f, w2s, xf, gf, b1, b2, bx, bg, lsem, ssem, rsem):
    net = Net(ssem, rsem)
    one = gather_w1(net, w1, w1f, b1, lsem)
    next(one)
    tokens = [gather_tokens(net, x, xf, bx, lsem.at[1]), gather_tokens(net, g, gf, bg, lsem.at[2])]
    for f in tokens:
        next(f)
    next(one)
    next(one)
    next(one)
    two = scatter_w2(net, w2, w2s, b2, lsem.at[3])
    run([one] + tokens + [two])
    net.finish()


def second_gather(w2s, act, g, w2f, act_l, g_l, b2, ba, bg, lsem, ssem, rsem):
    net = Net(ssem, rsem)
    acts = move_act(net, act, act_l, ba, lsem.at[1])
    next(acts)
    two = gather_w2(net, w2s, w2f, b2, lsem.at[0])
    next(two)
    toks = layer_tokens(net, g, lambda d: g, g_l, bg, lsem.at[2])
    run([two, acts, toks])
    net.finish()


def third_gather(d_pre, xf, ys, dxs, d_pre_l, x_l, yb, dxb, bd, bx, lsem, ssem, rsem):
    net = Net(ssem, rsem)
    rows, cols = bx.shape
    dp = gather_dpre(net, d_pre, d_pre_l, bd, lsem.at[0])
    next(dp)

    def piece(d):
        c = rot(net.x, d, NX)
        return xf.at[pl.ds(pl.multiple_of(net.k * rows, rows), rows), pl.ds(pl.multiple_of(c * cols, cols), cols)]

    toks = layer_tokens(net, piece(0), piece, x_l, bx, lsem.at[1])
    run([exchange_sums(net, ys, yb), exchange_sums(net, dxs, dxb), dp, toks])
    net.finish()


def comm(body, outs, bufs, n_local, n_remote, *args):
    hbm = pl.BlockSpec(memory_space=pltpu.HBM)
    return pl.pallas_call(
        body,
        out_shape=[jax.ShapeDtypeStruct(s, d) for s, d in outs],
        in_specs=[hbm] * len(args),
        out_specs=[hbm] * len(outs),
        scratch_shapes=[pltpu.VMEM(s, d) for s, d in bufs] + [
            pltpu.SemaphoreType.DMA((n_local,)), pltpu.SemaphoreType.DMA((n_remote,)), pltpu.SemaphoreType.DMA((n_remote,))],
        compiler_params=pltpu.CompilerParams(has_side_effects=True),
        cost_estimate=pl.CostEstimate(flops=80_000_000_000, bytes_accessed=64 << 20, transcendentals=0),
    )(*args)


def solution(mesh):
    act_spec = P(("dep", "row"), "col")
    wgt_spec = P("row", "col")
    grad_spec = P(("row", "dep"), "col")
    bf16, f32 = jnp.bfloat16, jnp.float32
    swap = [(r, r ^ 1) for r in range(2 * NX)]

    def dot(a, b, dims):
        return lax.dot_general(a, b, (dims, ((), ())), preferred_element_type=f32)

    def local_block(x_loc, w_up, w_down, g_loc):
        tb, hb = x_loc.shape
        hr, fb = w_up.shape
        fk = fb // 2
        hid = NY * hb
        tok = 2 * tb
        k = lax.rem(lax.axis_index("row"), 2)
        y = lax.axis_index("col")

        w1f, w2s, xf, gf = comm(
            first_gather,
            [((2 * NX * hr, fk), bf16), ((fk // 8, hid), bf16), ((tok, hid), bf16), ((tok, hid), bf16)],
            [((hr, fk), bf16), ((fk // 8, hb), bf16), ((tb, hb), bf16), ((tb, hb), bf16)], 4, 32,
            w_up, w_down, x_loc, g_loc)
        pre_act = dot(xf, w1f, ((1,), (0,)))
        act = gelu_fwd(pre_act).astype(bf16)
        w2f, act_l, g_l = comm(
            second_gather,
            [((fk, hid), bf16), ((NX, 4, tok // 4, fk), bf16), ((2 * NX, tb, hb), bf16)],
            [((fk // 8, hid), bf16), ((tok // 4, fk), bf16), ((tb, hb), bf16)], 3, 40,
            w2s, act, g_loc)
        d_act = dot(gf, w2f, ((1,), (1,)))
        d_pre = (d_act * gelu_slope(pre_act)).astype(bf16)
        dw_down_part = dot(act_l.reshape(NX * tok, fk), g_l.reshape(NX * tok, hb), ((0,), (0,)))
        dw_down = lax.psum_scatter(dw_down_part, "dep", scatter_dimension=0, tiled=True)

        def core_sum(part):
            keep = lax.dynamic_slice_in_dim(part, k * tb, tb, 0)
            give = lax.dynamic_slice_in_dim(part, (1 - k) * tb, tb, 0)
            return keep + lax.ppermute(give, "row", swap)

        ys = core_sum(dot(act, w2f, ((1,), (0,))))
        dxs = core_sum(dot(d_pre, w1f, ((1,), (1,))))
        d_pre, dw_down_part = lax.optimization_barrier((d_pre, dw_down_part))
        d_pre_l, x_l, yb, dxb = comm(
            third_gather,
            [((NX, tok, fk), bf16), ((2 * NX, tb, hb), bf16), ((3, tb, hb), f32), ((3, tb, hb), f32)],
            [((tok, fk), bf16), ((tb, hb), bf16)], 2, 32,
            d_pre, xf, ys, dxs)

        def col_sum(own, others):
            return (lax.dynamic_slice_in_dim(own, y * hb, hb, 1) + others[0] + others[1] + others[2]).astype(bf16)

        d_pre_l = d_pre_l.reshape(NX * tok, fk)
        x_l = x_l.reshape(NX * tok, hb)
        sums = []
        for c in range(2):
            part = dot(x_l[:, c * hr:(c + 1) * hr], d_pre_l, ((0,), (0,)))
            sums.append(lax.psum_scatter(part, "dep", scatter_dimension=0, tiled=True))
        keep = jnp.where(k == 0, sums[0], sums[1])
        take = lax.ppermute(jnp.where(k == 0, sums[1], sums[0]), "row", swap)
        dw_up = jnp.concatenate([jnp.where(k == 0, keep, take), jnp.where(k == 0, take, keep)], axis=1)
        return col_sum(ys, yb), col_sum(dxs, dxb), dw_up, dw_down

    return jax.shard_map(local_block, mesh=mesh, in_specs=(act_spec, wgt_spec, wgt_spec, act_spec), out_specs=(act_spec, act_spec, grad_spec, grad_spec), check_vma=False)
```

time: 1010 us -> 810 us (0.80)
  waiting for transfers between devices: 814 us -> 157 us
  Pallas kernels: 0 us -> 512 us
  blocking collectives: 54.1 us -> 0 us
  other arithmetic: 2.1 us -> 20.7 us
  matrix products: 105 us -> 94 us
    pallas_call x0 -> x3, Pallas kernels: none -> 512 us  [comm(): pl.pallas_call(body, out_shape=[jax.ShapeDtypeStruct(s, d) for s, d in ou...]
    all_gather x6 -> x0, waiting for transfers between devices: 483 us -> none  [the longest x1 160 us: local_block(): w_down_cols = lax.all_gather(w_down_loc, 'row', axis=0, tiled=True)]
    reduce_scatter x3 -> x2, waiting for transfers between devices: 186 us -> 83.3 us  [local_block(): sums.append(lax.psum_scatter(part, 'dep', scatter_dimension=0, tiled=True))]
    all_to_all x1 -> x0, waiting for transfers between devices: 61.3 us -> none  [local_block(): act_layer = lax.all_to_all(act_full, 'row', 1, 0, tiled=True)]
    all_to_all x1 -> x0, blocking collectives: 54.1 us -> none  [local_block(): x_layer = lax.all_to_all(x_full, 'row', 1, 0, tiled=True)]
    add x0 -> x2, other arithmetic: none -> 11.1 us  [core_sum(): return keep + lax.ppermute(give, 'row', swap)]
    dot_general x6 -> x7, matrix products: 105 us -> 94 us  [dot(): return lax.dot_general(a, b, (dims, ((), ())), preferred_element_type=f32)]
    all_to_all x2 -> x0, local copies, waits for them, and re-layouts: 10.7 us -> none  [the longest x1 8.27 us: local_block(): act_layer = lax.all_to_all(act_full, 'row', 1, 0, tiled=True)]
  transfers between devices with their start and end apart: 11 -> 6, of which waited for: 10 -> 3; matrix products, arithmetic and copies ran while one was open for 10% -> 9% of each run, Pallas kernels for 0% -> 0%
where the time goes in v1:
time: 810 us
  Pallas kernels  512 us (63%)
  waiting for transfers between devices  157 us (19%)
  matrix products  94 us (12%)
  other arithmetic  20.7 us (3%)
  between operations  13.9 us (2%)
  local copies, waits for them, and re-layouts  10.2 us (1%)
    pallas_call x3, Pallas kernels, comm(): pl.pallas_call(body, out_shape=[jax.ShapeDtypeStruct(s, d) for s, d in ou...  512 us
    dot_general x7, matrix products, dot(): return lax.dot_general(a, b, (dims, ((), ())), preferred_element_type=f32)  94 us
    reduce_scatter x2, waiting for transfers between devices, local_block(): sums.append(lax.psum_scatter(part, 'dep', scatter_dimension=0, tiled=True))  83.3 us
    reduce_scatter x1, waiting for transfers between devices, local_block(): lax.psum_scatter(dw_down_part, 'dep', scatter_dimension=0, tiled=True)  72.8 us
  transfers between devices with their start and end apart: 6, of which 3 were waited for; matrix products, arithmetic and copies ran while one was open for 9% of the time, Pallas kernels for 0%

profile of v1, /device:TPU:1, one launch (start us, length us, event | category | flops | bytes accessed | tf_op | source)
XLA Modules:
  0.0 809.7 jit_solution(4300745737319934427)
XLA Ops:
  7.2 115.6 %shard_map.75 = (bf16[4096,2048]{1,0:T(8,128)(2,1)}, bf16[256,4096]{1,0:T(8,128)(2,1)}, bf16[512,4096]{1,0:T(8,128)(2,1)}, bf16[512,4096]{1,0:T(8,128)(2,1)}) custom-call(bf16[512,4096]{1,0:T(8,128)(2,1)} %w1.1, bf16[2048,1024]{1,0:T(8,128)(2,1)} %w2.1, bf16[256,1024]{1,0:T(8,128)(2,1)} %x.1, bf16[256,1024]{1,0:T(8,128)(2,1)} %g.3), custom_call_target="tpu_custom_call" | custom-call | flops 80000000000 | bytes 67108864 | tf_op jit(solution)/shard_map/pallas_call | solution.py:344
  122.8 15.9 %multiply_convert_fusion = (bf16[512,2048]{1,0:T(8,128)(2,1)}, f32[512,2048]{1,0:T(8,128)}) fusion(bf16[512,4096]{1,0:T(8,128)(2,1)} %get-tuple-element.16.xf, bf16[4096,2048]{1,0:T(8,128)(2,1)} %get-tuple-element.17), kind=kOutput, calls=%fused_computation.11 | convolution fusion | flops 8599371776 | bytes 27262976 | tf_op jit(solution)/shard_map/dot_general | solution.py:364
  138.8 263.5 %shard_map.76 = (bf16[2048,4096]{1,0:T(8,128)(2,1)}, bf16[4,4,128,2048]{3,2,1,0:T(8,128)(2,1)}, bf16[8,256,1024]{2,1,0:T(8,128)(2,1)}) custom-call(bf16[256,4096]{1,0:T(8,128)(2,1)} %get-tuple-element.18.w2s, bf16[512,2048]{1,0:T(8,128)(2,1)} %get-tuple-element.30.act, bf16[256,1024]{1,0:T(8,128)(2,1)} %g.3), custom_call_target="tpu_custom_call" | custom-call | flops 80000000000 | bytes 67108864 | tf_op jit(solution)/shard_map/pallas_call | solution.py:344
  402.3 14.3 %fusion.13 = f32[512,4096]{1,0:T(8,128)} fusion(bf16[512,2048]{1,0:T(8,128)(2,1)S(1)} %copy-done.7, bf16[2048,4096]{1,0:T(8,128)(2,1)} %get-tuple-element.19), kind=kOutput, calls=%fused_computation.31 | convolution fusion | flops 8589934592 | bytes 27262976 | tf_op jit(solution)/shard_map/dot_general | solution.py:364
  416.6 4.8 constant_dynamic-slice_fusion.1
  421.4 0.9 collective-permute-start
  422.3 15.5 %fusion.6.d_pre = bf16[512,2048]{1,0:T(8,128)(2,1)S(1)} fusion(f32[512,2048]{1,0:T(8,128)S(1)} %copy-done.6, bf16[512,4096]{1,0:T(8,128)(2,1)} %get-tuple-element.20, bf16[2048,4096]{1,0:T(8,128)(2,1)} %get-tuple-element.19), kind=kOutput, calls=%fused_computation.8 | convolution fusion | flops 8609857536 | bytes 27262976 | tf_op jit(solution)/shard_map/dot_general | solution.py:364
  437.9 12.5 %fusion.15 = f32[512,4096]{1,0:T(8,128)S(1)} fusion(bf16[512,2048]{1,0:T(8,128)(2,1)S(1)} %fusion.6.d_pre, bf16[4096,2048]{1,0:T(8,128)(2,1)} %get-tuple-element.17), kind=kOutput, calls=%fused_computation.33 | convolution fusion | flops 8589934592 | bytes 27262976 | tf_op jit(solution)/shard_map/dot_general | solution.py:364
  450.4 2.5 constant_dynamic-slice_fusion
  452.9 2.0 copy-done
  454.9 14.6 %fusion.14 = f32[2048,1024]{1,0:T(8,128)} fusion(bf16[2048,2048]{1,0:T(8,128)(2,1)} %bitcast.40, bf16[2048,1024]{1,0:T(8,128)(2,1)} %bitcast.43), kind=kOutput, calls=%fused_computation.32 | convolution fusion | flops 8589934592 | bytes 20971520 | tf_op jit(solution)/shard_map/dot_general | solution.py:364
  469.5 6.3 dynamic-slice_add_fusion.1.ys
  476.7 4.7 dynamic-slice_add_fusion.dxs
  481.4 132.8 %shard_map.77 = (bf16[4,512,2048]{2,1,0:T(8,128)(2,1)}, bf16[8,256,1024]{2,1,0:T(8,128)(2,1)}, f32[3,256,1024]{2,1,0:T(8,128)}, f32[3,256,1024]{2,1,0:T(8,128)}) custom-call(bf16[512,2048]{1,0:T(8,128)(2,1)} %copy-done.5, bf16[512,4096]{1,0:T(8,128)(2,1)} %get-tuple-element.16.xf, f32[256,4096]{1,0:T(8,128)} %dynamic-slice_add_fusion.1.ys, ...), custom_call_target="tpu_custom_call" | custom-call | flops 80000000000 | bytes 67108864 | tf_op jit(solution)/shard_map/pallas_call | solution.py:344
  614.2 10.6 %fusion.7 = f32[512,2048]{1,0:T(8,128)} fusion(bf16[2048,2048]{1,0:T(8,128)(2,1)} %bitcast.41, bf16[2048,1024]{1,0:T(8,128)(2,1)} %bitcast.44), kind=kOutput, calls=%fused_computation.12 | convolution fusion | flops 4294967296 | bytes 14680064 | tf_op jit(solution)/shard_map/dot_general | solution.py:364
  625.1 10.6 %fusion.9 = f32[512,2048]{1,0:T(8,128)} fusion(bf16[2048,2048]{1,0:T(8,128)(2,1)} %bitcast.42, bf16[2048,1024]{1,0:T(8,128)(2,1)} %bitcast.45), kind=kOutput, calls=%fused_computation.14 | convolution fusion | flops 4294967296 | bytes 14680064 | tf_op jit(solution)/shard_map/dot_general | solution.py:364
  636.5 34.2 %reduce-scatter.6.cloned.1.call-done = f32[128,2048]{1,0:T(8,128)} async-done(((f32[512,2048]{1,0:T(8,128)}), f32[128,2048]{1,0:T(8,128)}) %reduce-scatter.6.cloned.1.call-update) | async-done | bytes 1048592 | tf_op jit(solution)/shard_map/reduce_scatter | solution.py:414
  670.7 49.1 %reduce-scatter.4.cloned.1.call-done = f32[128,2048]{1,0:T(8,128)} async-done(((f32[512,2048]{1,0:T(8,128)}), f32[128,2048]{1,0:T(8,128)}) %reduce-scatter.4.cloned.1.call-update) | async-done | bytes 1048592 | tf_op jit(solution)/shard_map/reduce_scatter | solution.py:414
  719.8 2.3 broadcast_select_fusion.2
  722.1 0.9 collective-permute-start.2
  723.0 4.4 fusion.11
  727.4 1.5 broadcast_select_fusion.1
  728.9 1.5 pad_maximum_fusion
  730.4 72.8 %reduce-scatter.8.cloned.1.call-done = f32[512,1024]{1,0:T(8,128)} async-done(((f32[2048,1024]{1,0:T(8,128)}), f32[512,1024]{1,0:T(8,128)}) %reduce-scatter.8.cloned.1.call-update) | async-done | bytes 2097168 | tf_op jit(solution)/shard_map/reduce_scatter | solution.py:390
  (25 shorter events, 2.0 us)
Async XLA Ops:
  7.2 663.5 %reduce-scatter.6.cloned.1.call-start = ((), (), s32[]{:S(2)}) async-start(), calls=%async_computation.4 | async-start | bytes 5242880 | tf_op jit(solution)/shard_map/reduce_scatter | solution.py:414
  138.8 263.5 %copy-start.7 = (bf16[512,2048]{1,0:T(8,128)(2,1)S(1)}, bf16[512,2048]{1,0:T(8,128)(2,1)}, u32[]{:S(2)}) copy-start(bf16[512,2048]{1,0:T(8,128)(2,1)} %get-tuple-element.30.act) | copy-start | bytes 6291460
  416.6 5.7 copy-start.6
  421.4 48.1 %collective-permute-start = (f32[256,4096]{1,0:T(8,128)}, f32[256,4096]{1,0:T(8,128)}, u32[]{:S(2)}, u32[]{:S(2)}) collective-permute-start(f32[256,4096]{1,0:T(8,128)} %constant_dynamic-slice_fusion.1), channel_id=1, source_target_pairs={{0,1},{1,0},{2,3},{3,2},{4,5},{5,4},{6,7},{7,6},{8,9},{9,8},{10,11... | collective-permute-start | bytes 12582920 | tf_op jit(solution)/shard_map/ppermute | solution.py:395
  437.9 12.5 %copy-start.5 = (bf16[512,2048]{1,0:T(8,128)(2,1)}, bf16[512,2048]{1,0:T(8,128)(2,1)S(1)}, u32[]{:S(2)}) copy-start(bf16[512,2048]{1,0:T(8,128)(2,1)S(1)} %fusion.6.d_pre) | copy-start | bytes 6291460
  450.4 4.5 copy-start
  454.9 21.0 %collective-permute-start.1 = (f32[256,4096]{1,0:T(8,128)}, f32[256,4096]{1,0:T(8,128)}, u32[]{:S(2)}, u32[]{:S(2)}) collective-permute-start(f32[256,4096]{1,0:T(8,128)} %constant_dynamic-slice_fusion), channel_id=1, source_target_pairs={{0,1},{1,0},{2,3},{3,2},{4,5},{5,4},{6,7},{7,6},{8,9},{9,8},{10,11... | collective-permute-start | bytes 12582920 | tf_op jit(solution)/shard_map/ppermute | solution.py:395
  469.5 7.3 copy-start.1
  624.8 95.0 %reduce-scatter.4.cloned.1.call-start = ((), (), s32[]{:S(2)}) async-start(), calls=%async_computation.3 | async-start | bytes 5242880 | tf_op jit(solution)/shard_map/reduce_scatter | solution.py:414
  635.7 87.3 %copy-start.4 = (f32[3,256,1024]{2,1,0:T(8,128)S(1)}, f32[3,256,1024]{2,1,0:T(8,128)}, u32[]{:S(2)}) copy-start(f32[3,256,1024]{2,1,0:T(8,128)} %get-tuple-element.24) | copy-start | bytes 9437188
  635.7 167.5 %reduce-scatter.8.cloned.1.call-start = ((), (), s32[]{:S(2)}) async-start(), calls=%async_computation.5 | async-start | bytes 10485760 | tf_op jit(solution)/shard_map/reduce_scatter | solution.py:390
  722.1 5.3 collective-permute-start.2
  723.0 4.4 copy-start.2
  723.0 4.4 copy-start.3
Sparse Core Ops, SparseCore 0:
  624.9 45.7 reduce-scatter.5
  673.1 46.6 reduce-scatter.3
  722.8 80.3 reduce-scatter.7

commit v2 on v1

v2 whole, which is shorter than its diff:
```python
import jax
import jax.numpy as jnp
from jax import lax
from jax.experimental import pallas as pl
from jax.experimental.pallas import tpu as pltpu
from jax.sharding import PartitionSpec as P

GELU_COEF = 0.7978845608028654
CUBIC_COEF = 0.044715
NX = 4
NY = 4
NZ = 4


def gelu_fwd(pre_act):
    inner = GELU_COEF * (pre_act + CUBIC_COEF * pre_act * pre_act * pre_act)
    return 0.5 * pre_act * (1.0 + jnp.tanh(inner))


def gelu_slope(pre_act):
    inner = GELU_COEF * (pre_act + CUBIC_COEF * pre_act * pre_act * pre_act)
    tanh_val = jnp.tanh(inner)
    return 0.5 * (1.0 + tanh_val) + 0.5 * pre_act * (1.0 - tanh_val * tanh_val) * GELU_COEF * (1.0 + 3.0 * CUBIC_COEF * pre_act * pre_act)


def rot(v, d, n):
    return lax.rem(v + (d % n), n)


class Net:
    def __init__(self, send_sem, recv_sem):
        self.send_sem, self.recv_sem = send_sem, recv_sem
        self.used = 0
        self.sent = []
        self.z = lax.axis_index("dep")
        self.y = lax.axis_index("col")
        row = lax.axis_index("row")
        self.row = row
        self.x = lax.div(row, 2)
        self.k = lax.rem(row, 2)

    def slots(self, n):
        base = self.used
        self.used += n
        return base

    def make(self, src, dst, where, send_slot, recv_slot):
        return pltpu.make_async_remote_copy(
            src_ref=src, dst_ref=dst, send_sem=self.send_sem.at[send_slot], recv_sem=self.recv_sem.at[recv_slot],
            device_id=where, device_id_type=pl.DeviceIdType.MESH)

    def send(self, src, dst, where):
        slot = self.slots(1)
        copy = self.make(src, dst, where, slot, slot)
        copy.start()
        self.sent.append(copy)
        return copy

    def finish(self):
        for copy in self.sent:
            copy.wait_send()

    def at_x(self, d):
        return {"row": 2 * rot(self.x, d, NX) + self.k}

    def at_y(self, d):
        return {"col": rot(self.y, d, NY)}

    def at_z(self, d):
        return {"dep": rot(self.z, d, NZ)}

    def partner(self):
        return {"row": 2 * self.x + 1 - self.k}


def ring(net, place, n, up, down, own, view, arrived, pieces=2):
    west, east, far = rot(place, -1, n), rot(place, 1, n), rot(place, 2, n)
    ups, downs, relays = [], [], []
    for q in range(pieces):
        if q == pieces // 2:
            yield
        r = pieces - 1 - q
        ups.append(net.send(own(q), view(place, q), up))
        downs.append(net.send(own(r), view(place, r), down))
    for q in range(pieces):
        yield
        r = pieces - 1 - q
        ups[q].wait_recv()
        if q < pieces // 2:
            relays.append((q, net.send(view(west, q), view(west, q), up)))
        arrived(west, q)
        downs[q].wait_recv()
        if q < pieces // 2:
            relays.append((r, net.send(view(east, r), view(east, r), down)))
        arrived(east, r)
    for q, copy in relays:
        yield
        copy.wait_recv()
        arrived(far, q)


def exchange(net, place, n, up, down, piece, slot, tmp, arrived=lambda j: None):
    west, east, far = rot(place, -1, n), rot(place, 1, n), rot(place, 2, n)
    lo = net.send(piece(far, 0), tmp.at[0], up)
    hi = net.send(piece(far, 1), tmp.at[1], down)
    e = net.send(piece(east, None), slot(place, 0, None), up)
    w = net.send(piece(west, None), slot(place, 1, None), down)
    yield
    lo.wait_recv()
    lo = net.send(tmp.at[0], slot(west, 2, 0), up)
    hi.wait_recv()
    hi = net.send(tmp.at[1], slot(east, 2, 1), down)
    yield
    e.wait_recv()
    arrived(west)
    w.wait_recv()
    arrived(east)
    yield
    lo.wait_recv()
    hi.wait_recv()
    arrived(far)


def rows_of(base, size, h):
    return pl.ds(base, size) if h is None else pl.ds(base + h * (size // 2), size // 2)


def to_z(net, view, got, pieces):
    def arrived(i, q):
        got.append(net.send(view(i, q), view(i, q), net.at_z(1 if q < pieces // 2 else -1)))
    return arrived


def gather_w1(net, w1, w1f, buf, sem):
    rows, cols = w1.shape[0], w1f.shape[1]
    size = rows // 4
    parity = lax.rem(net.z, 2)
    mine = pl.ds(pl.multiple_of(net.k * cols, cols), cols)
    other = pl.ds(pl.multiple_of((1 - net.k) * cols, cols), cols)
    own_rows = pl.ds(pl.multiple_of(net.row * rows, rows), rows)
    load = pltpu.make_async_copy(w1.at[:, mine], buf, sem)
    load.start()
    swap = net.send(w1.at[:, other], w1f.at[own_rows, :], net.partner())
    yield
    load.wait()
    store = pltpu.make_async_copy(buf, w1f.at[own_rows, :], sem)
    store.start()
    swap.wait_recv()
    store.wait()

    def view(i, q):
        return w1f.at[pl.ds(pl.multiple_of((2 * i + parity) * rows + q * size, size), size), :]

    got = []
    yield from ring(net, net.x, NX, net.at_x(1), net.at_x(-1), lambda q: view(net.x, q), view, to_z(net, view, got, 4), 4)
    yield
    for copy in got:
        copy.wait_recv()


def gather_tokens(net, src, dst, buf, sem):
    rows, cols = src.shape
    base = pl.multiple_of(net.k * rows, rows)

    def view(j, h):
        return dst.at[rows_of(base, rows, h), pl.ds(pl.multiple_of(j * cols, cols), cols)]

    load = pltpu.make_async_copy(src, buf, sem)
    load.start()
    passed = [net.send(src, view(net.y, None), net.partner())]

    def arrived(j, h):
        passed.append(net.send(view(j, h), view(j, h), net.partner()))

    gather = ring(net, net.y, NY, net.at_y(1), net.at_y(-1), lambda h: src.at[rows_of(0, rows, h), :], view, arrived)
    next(gather)
    load.wait()
    store = pltpu.make_async_copy(buf, view(net.y, None), sem)
    store.start()
    yield from gather
    yield
    store.wait()
    for copy in passed:
        copy.wait_recv()


def move_w2(net, w2, w2s, mid, tx, ty, sem):
    rows, cols = w2.shape
    part = rows // 8
    base = pl.multiple_of(lax.rem(net.z, 2) * 4 * part, part)

    def piece(i, h):
        return w2.at[rows_of(pl.multiple_of(base + i * part, part), part, h), :]

    load = pltpu.make_async_copy(piece(net.x, None), mid.at[net.x], sem)
    load.start()
    yield from exchange(net, net.x, NX, net.at_x(1), net.at_x(-1), piece, lambda j, side, h: mid.at[j, rows_of(0, part, h), :], tx)
    load.wait()

    def slot(j, side, h):
        return w2s.at[rows_of(0, part, h), pl.ds(pl.multiple_of(j * cols, cols), cols)]

    store = pltpu.make_async_copy(mid.at[net.y], slot(net.y, 0, None), sem)
    store.start()
    yield from exchange(net, net.y, NY, net.at_y(1), net.at_y(-1), lambda i, h: mid.at[i, rows_of(0, part, h), :], slot, ty)
    store.wait()


def gather_w2(net, w2s, w2f, buf, sem):
    rows = w2s.shape[0]
    size = rows // 4
    base = lax.rem(net.z, 2) * 4 * rows
    load = pltpu.make_async_copy(w2s, buf, sem)
    load.start()

    def view(i, q):
        return w2f.at[pl.ds(pl.multiple_of(base + i * rows + q * size, size), size), :]

    def own(q):
        return w2s.at[pl.ds(q * size, size), :]

    got = []
    gather = ring(net, net.x, NX, net.at_x(1), net.at_x(-1), own, view, to_z(net, view, got, 4), 4)
    next(gather)
    for q in (0, 3, 1, 2):
        got.append(net.send(own(q), view(net.x, q), net.at_z(1 if q < 2 else -1)))
    load.wait()
    store = pltpu.make_async_copy(buf, w2f.at[pl.ds(pl.multiple_of(base + net.x * rows, rows), rows), :], sem)
    store.start()
    yield
    yield from gather
    yield
    for copy in got:
        copy.wait_recv()
    store.wait()


def move_act(net, act, act_l, mid, tx, ty, sem):
    part = act_l.shape[2]

    def piece(i, h):
        return act.at[rows_of(pl.multiple_of(i * part, part), part, h), :]

    load = pltpu.make_async_copy(piece(net.y, None), mid.at[net.y], sem)
    load.start()
    yield from exchange(net, net.y, NY, net.at_y(1), net.at_y(-1), piece, lambda j, side, h: mid.at[j, rows_of(0, part, h), :], ty)
    load.wait()
    store = pltpu.make_async_copy(mid.at[net.x], act_l.at[net.x, net.y], sem)
    store.start()
    yield from exchange(
        net, net.x, NX, net.at_x(1), net.at_x(-1), lambda i, h: mid.at[i, rows_of(0, part, h), :],
        lambda j, side, h: act_l.at[j, net.y, rows_of(0, part, h), :], tx)
    store.wait()

    def view(j, h):
        return act_l.at[pl.ds(2 * h, 2), j]

    yield from ring(net, net.y, NY, net.at_y(1), net.at_y(-1), lambda h: view(net.y, h), view, lambda i, h: None)


def layer_g(net, g, g_l, buf, sem):
    rows = g.shape[0]
    load = pltpu.make_async_copy(g, buf, sem)
    load.start()

    def view(i, h):
        return g_l.at[2 * i + net.k, rows_of(0, rows, h), :]

    passed = [net.send(g, view(net.x, None), net.partner())]

    def arrived(i, h):
        passed.append(net.send(view(i, h), view(i, h), net.partner()))

    gather = ring(net, net.x, NX, net.at_x(1), net.at_x(-1), lambda h: g.at[rows_of(0, rows, h), :], view, arrived)
    next(gather)
    load.wait()
    store = pltpu.make_async_copy(buf, view(net.x, None), sem)
    store.start()
    yield from gather
    yield
    store.wait()
    for copy in passed:
        copy.wait_recv()


def layer_x(net, xf, x_l, buf, tmp, sem):
    rows, cols = buf.shape
    base = pl.multiple_of(net.k * rows, rows)

    def piece(i, h):
        return xf.at[rows_of(base, rows, h), pl.ds(pl.multiple_of(i * cols, cols), cols)]

    def slot(j, side, h):
        return x_l.at[2 * j + net.k, rows_of(0, rows, h), :]

    load = pltpu.make_async_copy(piece(net.x, None), buf, sem)
    load.start()
    own = slot(net.x, 0, None)
    passed = [net.send(piece(net.x, None), own, net.partner())]

    def arrived(j):
        passed.append(net.send(slot(j, 0, None), slot(j, 0, None), net.partner()))

    moves = exchange(net, net.x, NX, net.at_x(1), net.at_x(-1), piece, slot, tmp, arrived)
    next(moves)
    load.wait()
    store = pltpu.make_async_copy(buf, own, sem)
    store.start()
    yield
    yield from moves
    yield
    store.wait()
    for copy in passed:
        copy.wait_recv()


def gather_dpre(net, d_pre, col, d_pre_l, buf, sem):
    rows, cols = buf.shape
    cs = pl.ds(col * cols, cols)
    load = pltpu.make_async_copy(d_pre.at[:, cs], buf, sem)
    load.start()
    size = rows // 4

    def view(i, q):
        return d_pre_l.at[i, pl.ds(q * size, size), :]

    gather = ring(
        net, net.x, NX, net.at_x(1), net.at_x(-1), lambda q: d_pre.at[pl.ds(q * size, size), cs], view, lambda i, q: None, 4)
    next(gather)
    next(gather)
    load.wait()
    store = pltpu.make_async_copy(buf, d_pre_l.at[net.x], sem)
    store.start()
    yield
    yield from gather
    store.wait()


def exchange_sums(net, part, dst, tmp):
    rows, cols = dst.shape[1:]

    def piece(i, h):
        return part.at[rows_of(0, rows, h), pl.ds(pl.multiple_of(i * cols, cols), cols)]

    yield from exchange(
        net, net.y, NY, net.at_y(1), net.at_y(-1), piece, lambda j, side, h: dst.at[side, rows_of(0, rows, h), :], tmp)


def run(flows):
    flows = list(flows)
    while flows:
        flows = [f for f in flows if next(f, flows) is not flows]


def first_gather(w1, w2, x, g, w1f, w2s, xf, gf, b1, mid, tx, ty, bx, bg, lsem, ssem, rsem):
    net = Net(ssem, rsem)
    one = gather_w1(net, w1, w1f, b1, lsem.at[0])
    next(one)
    two = move_w2(net, w2, w2s, mid, tx, ty, lsem.at[3])
    next(two)
    next(one)
    tokens = [gather_tokens(net, x, xf, bx, lsem.at[1]), gather_tokens(net, g, gf, bg, lsem.at[2])]
    for f in tokens:
        next(f)
    next(two)
    next(one)
    run([two] + tokens + [one])
    net.finish()


def second_gather(w2s, act, g, w2f, act_l, g_l, b2, mid, tx, ty, bg, lsem, ssem, rsem):
    net = Net(ssem, rsem)
    acts = move_act(net, act, act_l, mid, tx, ty, lsem.at[1])
    next(acts)
    two = gather_w2(net, w2s, w2f, b2, lsem.at[0])
    next(two)
    next(acts)
    next(acts)
    next(acts)
    next(two)
    next(acts)
    toks = layer_g(net, g, g_l, bg, lsem.at[2])
    run([two, acts, toks])
    net.finish()


def third_gather(d_pre, xf, ys, d_pre_l, x_l, yb, bd, bx, tx, ty, lsem, ssem, rsem):
    net = Net(ssem, rsem)
    sums = exchange_sums(net, ys, yb, ty)
    next(sums)
    dp = gather_dpre(net, d_pre, 0, d_pre_l, bd, lsem.at[0])
    next(dp)
    toks = layer_x(net, xf, x_l, bx, tx, lsem.at[1])
    next(toks)
    run([dp, toks, sums])
    net.finish()


def fourth_gather(d_pre, dxs, d_pre_l, dxb, bd, ty, lsem, ssem, rsem):
    net = Net(ssem, rsem)
    sums = exchange_sums(net, dxs, dxb, ty)
    next(sums)
    dp = gather_dpre(net, d_pre, 1, d_pre_l, bd, lsem.at[0])
    run([dp, sums])
    net.finish()


def comm(body, outs, bufs, n_local, n_remote, *args):
    hbm = pl.BlockSpec(memory_space=pltpu.HBM)
    return pl.pallas_call(
        body,
        out_shape=[jax.ShapeDtypeStruct(s, d) for s, d in outs],
        in_specs=[hbm] * len(args),
        out_specs=[hbm] * len(outs),
        scratch_shapes=[pltpu.VMEM(s, d) for s, d in bufs] + [
            pltpu.SemaphoreType.DMA((n_local,)), pltpu.SemaphoreType.DMA((n_remote,)), pltpu.SemaphoreType.DMA((n_remote,))],
        compiler_params=pltpu.CompilerParams(has_side_effects=True),
        cost_estimate=pl.CostEstimate(flops=80_000_000_000, bytes_accessed=64 << 20, transcendentals=0),
    )(*args)


def solution(mesh):
    act_spec = P(("dep", "row"), "col")
    wgt_spec = P("row", "col")
    grad_spec = P(("row", "dep"), "col")
    bf16, f32 = jnp.bfloat16, jnp.float32
    swap = [(r, r ^ 1) for r in range(2 * NX)]

    def dot(a, b, dims):
        return lax.dot_general(a, b, (dims, ((), ())), preferred_element_type=f32)

    def local_block(x_loc, w_up, w_down, g_loc):
        tb, hb = x_loc.shape
        hr, fb = w_up.shape
        fk = fb // 2
        hid = NY * hb
        tok = 2 * tb
        k = lax.rem(lax.axis_index("row"), 2)
        y = lax.axis_index("col")

        w1f, w2s, xf, gf = comm(
            first_gather,
            [((2 * NX * hr, fk), bf16), ((fk // 8, hid), bf16), ((tok, hid), bf16), ((tok, hid), bf16)],
            [((hr, fk), bf16), ((4, fk // 8, hb), bf16), ((2, fk // 16, hb), bf16), ((2, fk // 16, hb), bf16),
             ((tb, hb), bf16), ((tb, hb), bf16)], 4, 80,
            w_up, w_down, x_loc, g_loc)
        pre_act = dot(xf, w1f, ((1,), (0,)))
        act = gelu_fwd(pre_act).astype(bf16)
        w2f, act_l, g_l = comm(
            second_gather,
            [((fk, hid), bf16), ((NX, 4, tok // 4, fk), bf16), ((2 * NX, tb, hb), bf16)],
            [((fk // 8, hid), bf16), ((4, tok // 4, fk), bf16), ((2, tok // 8, fk), bf16), ((2, tok // 8, fk), bf16),
             ((tb, hb), bf16)], 3, 80,
            w2s, act, g_loc)
        d_act = dot(gf, w2f, ((1,), (1,)))
        d_pre = (d_act * gelu_slope(pre_act)).astype(bf16)
        dw_down_part = dot(act_l.reshape(NX * tok, fk), g_l.reshape(NX * tok, hb), ((0,), (0,)))
        dw_down = lax.psum_scatter(dw_down_part, "dep", scatter_dimension=0, tiled=True)

        def core_sum(part):
            keep = lax.dynamic_slice_in_dim(part, k * tb, tb, 0)
            give = lax.dynamic_slice_in_dim(part, (1 - k) * tb, tb, 0)
            return keep + lax.ppermute(give, "row", swap)

        def col_sum(own, others):
            return (lax.dynamic_slice_in_dim(own, y * hb, hb, 1) + others[0] + others[1] + others[2]).astype(bf16)

        ys = core_sum(dot(act, w2f, ((1,), (0,))))
        d_pre, dw_down_part = lax.optimization_barrier((d_pre, dw_down_part))
        d_pre_l0, x_l, yb = comm(
            third_gather,
            [((NX, tok, fk // 2), bf16), ((2 * NX, tb, hb), bf16), ((3, tb, hb), f32)],
            [((tok, fk // 2), bf16), ((tb, hb), bf16), ((2, tb // 2, hb), bf16), ((2, tb // 2, hb), f32)], 2, 64,
            d_pre, xf, ys)
        x_l = x_l.reshape(NX * tok, 2, NZ, hr // NZ).transpose(0, 2, 1, 3).reshape(NX * tok, hb)

        def up_part(d_pre_l):
            return dot(x_l, d_pre_l.reshape(NX * tok, fk // 2), ((0,), (0,)))

        part0 = up_part(d_pre_l0)
        dxs = core_sum(dot(d_pre, w1f, ((1,), (1,))))
        d_pre, part0 = lax.optimization_barrier((d_pre, part0))
        d_pre_l1, dxb = comm(
            fourth_gather,
            [((NX, tok, fk // 2), bf16), ((3, tb, hb), f32)],
            [((tok, fk // 2), bf16), ((2, tb // 2, hb), f32)], 1, 40,
            d_pre, dxs)
        part0, dw_down = lax.optimization_barrier((part0, dw_down))
        outs = []
        for part in (part0, up_part(d_pre_l1)):
            total = lax.psum_scatter(part, "dep", scatter_dimension=0, tiled=True).reshape(2, hr // NZ, fk // 2)
            keep = jnp.where(k == 0, total[0], total[1])
            take = lax.ppermute(jnp.where(k == 0, total[1], total[0]), "row", swap)
            outs.append((jnp.where(k == 0, keep, take), jnp.where(k == 0, take, keep)))
        dw_up = jnp.concatenate([outs[0][0], outs[1][0], outs[0][1], outs[1][1]], axis=1)
        return col_sum(ys, yb), col_sum(dxs, dxb), dw_up, dw_down

    return jax.shard_map(local_block, mesh=mesh, in_specs=(act_spec, wgt_spec, wgt_spec, act_spec), out_specs=(act_spec, act_spec, grad_spec, grad_spec), check_vma=False)
```

time: 810 us -> 655 us (0.81)
  Pallas kernels: 512 us -> 402 us
  waiting for transfers between devices: 157 us -> 91 us
  local copies, waits for them, and re-layouts: 10.2 us -> 24.7 us
    pallas_call x3 -> x4, Pallas kernels: 512 us -> 402 us  [comm(): pl.pallas_call(body, out_shape=[jax.ShapeDtypeStruct(s, d) for s, d in ou...]
    reduce_scatter x1, waiting for transfers between devices: 72.8 us -> 0.02 us  [local_block(): lax.psum_scatter(dw_down_part, 'dep', scatter_dimension=0, tiled=True)]
    reshape x0 -> x2, local copies, waits for them, and re-layouts: none -> 15.2 us  [local_block(): x_l.reshape(NX * tok, 2, NZ, hr // NZ).transpose(0, 2, 1, 3)]
  transfers between devices with their start and end apart: 6 -> 7, of which waited for: 3 -> 2; matrix products, arithmetic and copies ran while one was open for 9% -> 16% of each run, Pallas kernels for 0% -> 19%
where the time goes in v2:
time: 655 us; the launch traced here: 654 us
  Pallas kernels  402 us (61%)
  matrix products  91.9 us (14%)
  waiting for transfers between devices  91 us (14%)
  local copies, waits for them, and re-layouts  24.7 us (4%)
  other arithmetic  24 us (4%)
  between operations  13.9 us (2%)
  starting transfers between devices  6.55 us (1%)
    pallas_call x4, Pallas kernels, comm(): pl.pallas_call(body, out_shape=[jax.ShapeDtypeStruct(s, d) for s, d in ou...  402 us
    dot_general x7, matrix products, dot(): return lax.dot_general(a, b, (dims, ((), ())), preferred_element_type=f32)  91.9 us
    reduce_scatter x2, waiting for transfers between devices, local_block(): lax.psum_scatter(part, 'dep', scatter_dimension=0, tiled=True)  90.2 us
    reshape x2, local copies, waits for them, and re-layouts, local_block(): x_l.reshape(NX * tok, 2, NZ, hr // NZ).transpose(0, 2, 1, 3)  15.2 us
  transfers between devices with their start and end apart: 7, of which 2 were waited for; matrix products, arithmetic and copies ran while one was open for 16% of the time, Pallas kernels for 19%

profile of v2, /device:TPU:1, one launch (start us, length us, event | category | flops | bytes accessed | tf_op | source)
XLA Modules:
  0.0 654.4 jit_solution(13800208571326637732)
XLA Ops:
  7.2 120.1 %shard_map.75 = (bf16[4096,2048]{1,0:T(8,128)(2,1)}, bf16[256,4096]{1,0:T(8,128)(2,1)}, bf16[512,4096]{1,0:T(8,128)(2,1)}, bf16[512,4096]{1,0:T(8,128)(2,1)}) custom-call(bf16[512,4096]{1,0:T(8,128)(2,1)} %w1.1, bf16[2048,1024]{1,0:T(8,128)(2,1)} %w2.1, bf16[256,1024]{1,0:T(8,128)(2,1)} %x.1, bf16[256,1024]{1,0:T(8,128)(2,1)} %g.3), custom_call_target="tpu_custom_call" | custom-call | flops 80000000000 | bytes 67108864 | tf_op jit(solution)/shard_map/pallas_call | solution.py:410
  127.3 15.9 %multiply_convert_fusion = (bf16[512,2048]{1,0:T(8,128)(2,1)}, f32[512,2048]{1,0:T(8,128)}) fusion(bf16[512,4096]{1,0:T(8,128)(2,1)} %get-tuple-element.21.xf, bf16[4096,2048]{1,0:T(8,128)(2,1)} %get-tuple-element.22), kind=kOutput, calls=%fused_computation.11 | convolution fusion | flops 8599371776 | bytes 27262976 | tf_op jit(solution)/shard_map/dot_general | solution.py:430
  143.3 160.9 %shard_map.76 = (bf16[2048,4096]{1,0:T(8,128)(2,1)}, bf16[4,4,128,2048]{3,2,1,0:T(8,128)(2,1)}, bf16[8,256,1024]{2,1,0:T(8,128)(2,1)}) custom-call(bf16[256,4096]{1,0:T(8,128)(2,1)} %get-tuple-element.23.w2s, bf16[512,2048]{1,0:T(8,128)(2,1)} %get-tuple-element.42.act, bf16[256,1024]{1,0:T(8,128)(2,1)} %g.3), custom_call_target="tpu_custom_call" | custom-call | flops 80000000000 | bytes 67108864 | tf_op jit(solution)/shard_map/pallas_call | solution.py:410
  304.2 14.4 %fusion.9 = f32[512,4096]{1,0:T(8,128)} fusion(bf16[512,2048]{1,0:T(8,128)(2,1)S(1)} %copy-done.6, bf16[2048,4096]{1,0:T(8,128)(2,1)} %get-tuple-element.24), kind=kOutput, calls=%fused_computation.31 | convolution fusion | flops 8589934592 | bytes 27262976 | tf_op jit(solution)/shard_map/dot_general | solution.py:430
  318.6 4.9 constant_dynamic-slice_fusion.1
  323.5 3.3 collective-permute-start
  326.8 13.2 %fusion.10 = f32[2048,1024]{1,0:T(8,128)} fusion(bf16[2048,2048]{1,0:T(8,128)(2,1)S(1)} %bitcast.47, bf16[2048,1024]{1,0:T(8,128)(2,1)} %bitcast.48), kind=kOutput, calls=%fused_computation.32 | convolution fusion | flops 8589934592 | bytes 20971520 | tf_op jit(solution)/shard_map/dot_general | solution.py:430
  340.0 16.1 %fusion.6.d_pre = bf16[512,2048]{1,0:T(8,128)(2,1)S(1)} fusion(f32[512,2048]{1,0:T(8,128)} %get-tuple-element.43, bf16[512,4096]{1,0:T(8,128)(2,1)} %get-tuple-element.25, bf16[2048,4096]{1,0:T(8,128)(2,1)} %get-tuple-element.24), kind=kOutput, calls=%fused_computation.8 | convolution fusion | flops 8609857536 | bytes 27262976 | tf_op jit(solution)/shard_map/dot_general | solution.py:430
  356.2 12.5 %fusion.11 = f32[512,4096]{1,0:T(8,128)S(1)} fusion(bf16[512,2048]{1,0:T(8,128)(2,1)S(1)} %fusion.6.d_pre, bf16[4096,2048]{1,0:T(8,128)(2,1)} %get-tuple-element.22), kind=kOutput, calls=%fused_computation.33 | convolution fusion | flops 8589934592 | bytes 27262976 | tf_op jit(solution)/shard_map/dot_general | solution.py:430
  368.7 2.5 constant_dynamic-slice_fusion
  371.1 2.1 copy-done
  374.4 6.1 dynamic-slice_add_fusion.1.ys
  380.5 64.7 %shard_map.77 = (bf16[4,512,1024]{2,1,0:T(8,128)(2,1)}, bf16[8,256,1024]{2,1,0:T(8,128)(2,1)}, f32[3,256,1024]{2,1,0:T(8,128)}) custom-call(bf16[512,2048]{1,0:T(8,128)(2,1)} %copy-done.5, bf16[512,4096]{1,0:T(8,128)(2,1)} %get-tuple-element.21.xf, f32[256,4096]{1,0:T(8,128)} %dynamic-slice_add_fusion.1.ys), custom_call_target="tpu_custom_call" | custom-call | flops 80000000000 | bytes 67108864 | tf_op jit(solution)/shard_map/pallas_call | solution.py:410
  445.2 7.7 %reshape.38 = bf16[2048,2,4,128]{3,2,1,0:T(4,128)(2,1)} reshape(bf16[8,256,1024]{2,1,0:T(8,128)(2,1)} %get-tuple-element.30) | data formatting | bytes 8388608 | tf_op jit(solution)/shard_map/reshape | solution.py:475
  452.9 7.5 %copy.8 = bf16[2048,2,4,128]{0,3,1,2:T(8,128)(2,1)} copy(bf16[2048,2,4,128]{3,2,1,0:T(4,128)(2,1)} %reshape.38) | data formatting | bytes 8388608 | tf_op jit(solution)/shard_map/reshape | solution.py:475
  460.4 9.9 %fusion.12 = f32[1024,1024]{1,0:T(8,128)} fusion(bf16[2048,1024]{0,1:T(8,128)(2,1)} %bitcast.45, bf16[2048,1024]{1,0:T(8,128)(2,1)} %bitcast.49), kind=kOutput, calls=%fused_computation.34 | convolution fusion | flops 4294967296 | bytes 12582912 | tf_op jit(solution)/shard_map/dot_general | solution.py:430
  470.3 6.1 dynamic-slice_add_fusion.dxs
  476.4 56.8 %shard_map.78 = (bf16[4,512,1024]{2,1,0:T(8,128)(2,1)}, f32[3,256,1024]{2,1,0:T(8,128)}) custom-call(bf16[512,2048]{1,0:T(8,128)(2,1)} %copy-done.5, f32[256,4096]{1,0:T(8,128)} %dynamic-slice_add_fusion.dxs), custom_call_target="tpu_custom_call" | custom-call | flops 80000000000 | bytes 67108864 | tf_op jit(solution)/shard_map/pallas_call | solution.py:410
  533.3 9.9 %fusion.13 = f32[1024,1024]{1,0:T(8,128)} fusion(bf16[2048,1024]{0,1:T(8,128)(2,1)} %bitcast.46, bf16[2048,1024]{1,0:T(8,128)(2,1)} %bitcast.50), kind=kOutput, calls=%fused_computation.35 | convolution fusion | flops 4294967296 | bytes 12582912 | tf_op jit(solution)/shard_map/dot_general | solution.py:430
  543.9 46.5 %reduce-scatter.8.cloned.1.call-done = f32[256,1024]{1,0:T(8,128)} async-done(((f32[1024,1024]{1,0:T(8,128)}), f32[256,1024]{1,0:T(8,128)}) %reduce-scatter.8.cloned.1.call-update) | async-done | bytes 1048592 | tf_op jit(solution)/shard_map/reduce_scatter | solution.py:491
  590.4 2.1 slice_select_fusion
  593.4 2.4 fusion.8
  595.7 43.7 %reduce-scatter.6.cloned.1.call-done = f32[256,1024]{1,0:T(8,128)} async-done(((f32[1024,1024]{1,0:T(8,128)}), f32[256,1024]{1,0:T(8,128)}) %reduce-scatter.6.cloned.1.call-update) | async-done | bytes 1048592 | tf_op jit(solution)/shard_map/reduce_scatter | solution.py:491
  641.8 3.3 fusion.7
  (31 shorter events, 8.1 us)
Async XLA Ops:
  7.2 536.1 %reduce-scatter.4.cloned.1.call-start = ((), (), s32[]{:S(2)}) async-start(), calls=%async_computation.3 | async-start | bytes 10485760 | tf_op jit(solution)/shard_map/reduce_scatter | solution.py:458
  143.3 160.9 %copy-start.6 = (bf16[512,2048]{1,0:T(8,128)(2,1)S(1)}, bf16[512,2048]{1,0:T(8,128)(2,1)}, u32[]{:S(2)}) copy-start(bf16[512,2048]{1,0:T(8,128)(2,1)} %get-tuple-element.42.act) | copy-start | bytes 6291460
  318.6 8.2 %copy-start.4 = (bf16[4,4,128,2048]{3,2,1,0:T(8,128)(2,1)S(1)}, bf16[4,4,128,2048]{3,2,1,0:T(8,128)(2,1)}, u32[]{:S(2)}) copy-start(bf16[4,4,128,2048]{3,2,1,0:T(8,128)(2,1)} %get-tuple-element.26) | copy-start | bytes 25165828
  323.5 50.9 %collective-permute-start = (f32[256,4096]{1,0:T(8,128)}, f32[256,4096]{1,0:T(8,128)}, u32[]{:S(2)}, u32[]{:S(2)}) collective-permute-start(f32[256,4096]{1,0:T(8,128)} %constant_dynamic-slice_fusion.1), channel_id=1, source_target_pairs={{0,1},{1,0},{2,3},{3,2},{4,5},{5,4},{6,7},{7,6},{8,9},{9,8},{10,11... | collective-permute-start | bytes 12582920 | tf_op jit(solution)/shard_map/ppermute | solution.py:463
  340.0 250.4 %reduce-scatter.8.cloned.1.call-start = ((), (), s32[]{:S(2)}) async-start(), calls=%async_computation.5 | async-start | bytes 5242880 | tf_op jit(solution)/shard_map/reduce_scatter | solution.py:491
  356.2 12.5 %copy-start.5 = (bf16[512,2048]{1,0:T(8,128)(2,1)}, bf16[512,2048]{1,0:T(8,128)(2,1)S(1)}, u32[]{:S(2)}) copy-start(bf16[512,2048]{1,0:T(8,128)(2,1)S(1)} %fusion.6.d_pre) | copy-start | bytes 6291460
  368.7 4.6 copy-start
  373.2 97.1 %collective-permute-start.1 = (f32[256,4096]{1,0:T(8,128)}, f32[256,4096]{1,0:T(8,128)}, u32[]{:S(2)}, u32[]{:S(2)}) collective-permute-start(f32[256,4096]{1,0:T(8,128)} %constant_dynamic-slice_fusion), channel_id=1, source_target_pairs={{0,1},{1,0},{2,3},{3,2},{4,5},{5,4},{6,7},{7,6},{8,9},{9,8},{10,11... | collective-permute-start | bytes 12582920 | tf_op jit(solution)/shard_map/ppermute | solution.py:463
  543.1 50.2 %copy-start.3 = (f32[3,256,1024]{2,1,0:T(8,128)S(1)}, f32[3,256,1024]{2,1,0:T(8,128)}, u32[]{:S(2)}) copy-start(f32[3,256,1024]{2,1,0:T(8,128)} %get-tuple-element.29) | copy-start | bytes 9437188
  543.2 96.3 %reduce-scatter.6.cloned.1.call-start = ((), (), s32[]{:S(2)}) async-start(), calls=%async_computation.4 | async-start | bytes 5242880 | tf_op jit(solution)/shard_map/reduce_scatter | solution.py:491
  592.5 52.7 %collective-permute-start.3 = (f32[128,1024]{1,0:T(8,128)}, f32[128,1024]{1,0:T(8,128)}, u32[]{:S(2)}, u32[]{:S(2)}) collective-permute-start(f32[128,1024]{1,0:T(8,128)} %slice_select_fusion), channel_id=1, source_target_pairs={{0,1},{1,0},{2,3},{3,2},{4,5},{5,4},{6,7},{7,6},{8,9},{9,8},{10,11... | collective-permute-start | bytes 1572872 | tf_op jit(solution)/shard_map/ppermute | solution.py:493
  595.7 49.4 %copy-start.1 = (f32[256,1024]{1,0:T(8,128)S(1)}, f32[256,1024]{1,0:T(8,128)}, u32[]{:S(2)}) copy-start(f32[256,1024]{1,0:T(8,128)} %reduce-scatter.8.cloned.1.call-done) | copy-start | bytes 3145732
  639.5 6.8 %copy-start.2 = (f32[256,1024]{1,0:T(8,128)S(1)}, f32[256,1024]{1,0:T(8,128)}, u32[]{:S(2)}) copy-start(f32[256,1024]{1,0:T(8,128)} %reduce-scatter.6.cloned.1.call-done) | copy-start | bytes 3145732
  640.8 5.5 collective-permute-start.2
Sparse Core Ops, SparseCore 0:
  340.1 78.0 reduce-scatter.3
  543.3 47.0 reduce-scatter.7
  592.8 46.6 reduce-scatter.5

commit v3 on v2

--- a/solution.py
+++ b/solution.py
@@ -137,19 +137,25 @@
     parity = lax.rem(net.z, 2)
     mine = pl.ds(pl.multiple_of(net.k * cols, cols), cols)
     other = pl.ds(pl.multiple_of((1 - net.k) * cols, cols), cols)
-    own_rows = pl.ds(pl.multiple_of(net.row * rows, rows), rows)
+
+    def slot(i, q, k):
+        return w1f.at[pl.ds(pl.multiple_of(i * 8 * size + q * 2 * size + k * size, size), size), :]
+
     load = pltpu.make_async_copy(w1.at[:, mine], buf, sem)
     load.start()
-    swap = net.send(w1.at[:, other], w1f.at[own_rows, :], net.partner())
+    swaps = [net.send(w1.at[pl.ds(q * size, size), other], slot(net.x, q, net.k), net.partner()) for q in range(4)]
     yield
     load.wait()
-    store = pltpu.make_async_copy(buf, w1f.at[own_rows, :], sem)
-    store.start()
-    swap.wait_recv()
-    store.wait()
+    stores = [pltpu.make_async_copy(buf.at[pl.ds(q * size, size), :], slot(net.x, q, net.k), sem) for q in range(4)]
+    for copy in stores:
+        copy.start()
+    for copy in swaps:
+        copy.wait_recv()
+    for copy in stores:
+        copy.wait()
 
     def view(i, q):
-        return w1f.at[pl.ds(pl.multiple_of((2 * i + parity) * rows + q * size, size), size), :]
+        return slot(i, q, parity)
 
     got = []
     yield from ring(net, net.x, NX, net.at_x(1), net.at_x(-1), lambda q: view(net.x, q), view, to_z(net, view, got, 4), 4)
@@ -158,15 +164,24 @@
         copy.wait_recv()
 
 
-def gather_tokens(net, src, dst, buf, sem):
+def gather_tokens(net, src, dst, buf, sem, order=None):
     rows, cols = src.shape
     base = pl.multiple_of(net.k * rows, rows)
 
     def view(j, h):
         return dst.at[rows_of(base, rows, h), pl.ds(pl.multiple_of(j * cols, cols), cols)]
 
-    load = pltpu.make_async_copy(src, buf, sem)
-    load.start()
+    if order is None:
+        loads = [pltpu.make_async_copy(src, buf, sem)]
+    else:
+        size = cols // len(order)
+        loads = [
+            pltpu.make_async_copy(src.at[:, pl.ds(b * size, size)], buf.at[:, pl.ds(n * size, size)], sem) for n, b in enumerate(order)]
+    for copy in loads:
+        copy.start()
+    for copy in loads:
+        copy.wait()
+    src = buf
     passed = [net.send(src, view(net.y, None), net.partner())]
 
     def arrived(j, h):
@@ -174,7 +189,6 @@
 
     gather = ring(net, net.y, NY, net.at_y(1), net.at_y(-1), lambda h: src.at[rows_of(0, rows, h), :], view, arrived)
     next(gather)
-    load.wait()
     store = pltpu.make_async_copy(buf, view(net.y, None), sem)
     store.start()
     yield from gather
@@ -206,12 +220,10 @@
     store.wait()
 
 
-def gather_w2(net, w2s, w2f, buf, sem):
+def gather_w2(net, w2s, w2f, sem):
     rows = w2s.shape[0]
     size = rows // 4
     base = lax.rem(net.z, 2) * 4 * rows
-    load = pltpu.make_async_copy(w2s, buf, sem)
-    load.start()
 
     def view(i, q):
         return w2f.at[pl.ds(pl.multiple_of(base + i * rows + q * size, size), size), :]
@@ -224,8 +236,7 @@
     next(gather)
     for q in (0, 3, 1, 2):
         got.append(net.send(own(q), view(net.x, q), net.at_z(1 if q < 2 else -1)))
-    load.wait()
-    store = pltpu.make_async_copy(buf, w2f.at[pl.ds(pl.multiple_of(base + net.x * rows, rows), rows), :], sem)
+    store = pltpu.make_async_copy(w2s, w2f.at[pl.ds(pl.multiple_of(base + net.x * rows, rows), rows), :], sem)
     store.start()
     yield
     yield from gather
@@ -235,25 +246,25 @@
     store.wait()
 
 
-def move_act(net, act, act_l, mid, tx, ty, sem):
+def move_act(net, act, act_l, cs, mid, tx, ty, sem):
     part = act_l.shape[2]
 
     def piece(i, h):
-        return act.at[rows_of(pl.multiple_of(i * part, part), part, h), :]
+        return act.at[rows_of(pl.multiple_of(i * part, part), part, h), cs]
 
     load = pltpu.make_async_copy(piece(net.y, None), mid.at[net.y], sem)
     load.start()
     yield from exchange(net, net.y, NY, net.at_y(1), net.at_y(-1), piece, lambda j, side, h: mid.at[j, rows_of(0, part, h), :], ty)
     load.wait()
-    store = pltpu.make_async_copy(mid.at[net.x], act_l.at[net.x, net.y], sem)
+    store = pltpu.make_async_copy(mid.at[net.x], act_l.at[net.x, net.y, :, cs], sem)
     store.start()
     yield from exchange(
         net, net.x, NX, net.at_x(1), net.at_x(-1), lambda i, h: mid.at[i, rows_of(0, part, h), :],
-        lambda j, side, h: act_l.at[j, net.y, rows_of(0, part, h), :], tx)
+        lambda j, side, h: act_l.at[j, net.y, rows_of(0, part, h), cs], tx)
     store.wait()
 
     def view(j, h):
-        return act_l.at[pl.ds(2 * h, 2), j]
+        return act_l.at[pl.ds(2 * h, 2), j, :, cs]
 
     yield from ring(net, net.y, NY, net.at_y(1), net.at_y(-1), lambda h: view(net.y, h), view, lambda i, h: None)
 
@@ -346,41 +357,111 @@
         net, net.y, NY, net.at_y(1), net.at_y(-1), piece, lambda j, side, h: dst.at[side, rows_of(0, rows, h), :], tmp)
 
 
+def exchange_layers(net, part, dst, tmp):
+    rows = dst.shape[1]
+
+    def piece(i, h):
+        return part.at[rows_of(pl.multiple_of(i * rows, rows), rows, h), :]
+
+    yield from exchange(
+        net, net.z, NZ, net.at_z(1), net.at_z(-1), piece, lambda j, side, h: dst.at[side, rows_of(0, rows, h), :], tmp)
+
+
 def run(flows):
     flows = list(flows)
     while flows:
         flows = [f for f in flows if next(f, flows) is not flows]
 
 
-def first_gather(w1, w2, x, g, w1f, w2s, xf, gf, b1, mid, tx, ty, bx, bg, lsem, ssem, rsem):
+def up_tiles(first, w1f, xv, wbuf, uv, av, wsem):
+    cols = wbuf.shape[2]
+
+    def fetch(i, slot):
+        t = pl.ds(pl.multiple_of((first + i) * cols, cols), cols)
+        return pltpu.make_async_copy(w1f.at[:, t], wbuf.at[slot], wsem.at[slot])
+
+    fetch(0, 0).start()
+
+    @pl.loop(0, 4)
+    def _(i):
+        slot = lax.rem(i, 2)
+
+        @pl.when(i < 3)
+        def _():
+            fetch(i + 1, 1 - slot).start()
+
+        fetch(i, slot).wait()
+        t = pl.ds(pl.multiple_of((first + i) * cols, cols), cols)
+        u = jnp.dot(xv[...], wbuf[slot], preferred_element_type=jnp.float32)
+        uv[:, t] = u
+        av[:, t] = gelu_fwd(u).astype(av.dtype)
+
+
+def steps(flow, n):
+    for _ in range(n):
+        next(flow, None)
+
+
+def first_kernel(
+        w1, w2, x, g, w1f, w2f, xf, gf, pre, act, act_l, g_l, b1, mid, tx, ty, bx, bg, bl, w2s, xv, wbuf, uv, av, mids, txa, tya,
+        lsem, wsem, ssem, rsem):
     net = Net(ssem, rsem)
+    cols = act.shape[1] // 2
+    chunks = [pl.ds(c * cols, cols) for c in range(2)]
     one = gather_w1(net, w1, w1f, b1, lsem.at[0])
-    next(one)
+    steps(one, 1)
+    tokens = [gather_tokens(net, x, xf, bx, lsem.at[1], [c * NZ + q for q in range(NZ) for c in range(2)]), gather_tokens(net, g, gf, bg, lsem.at[2])]
+    for f in tokens:
+        steps(f, 1)
+    steps(one, 2)
     two = move_w2(net, w2, w2s, mid, tx, ty, lsem.at[3])
-    next(two)
-    next(one)
-    tokens = [gather_tokens(net, x, xf, bx, lsem.at[1]), gather_tokens(net, g, gf, bg, lsem.at[2])]
+    steps(two, 1)
     for f in tokens:
-        next(f)
-    next(two)
-    next(one)
-    run([two] + tokens + [one])
-    net.finish()
-
-
-def second_gather(w2s, act, g, w2f, act_l, g_l, b2, mid, tx, ty, bg, lsem, ssem, rsem):
-    net = Net(ssem, rsem)
-    acts = move_act(net, act, act_l, mid, tx, ty, lsem.at[1])
-    next(acts)
-    two = gather_w2(net, w2s, w2f, b2, lsem.at[0])
-    next(two)
-    next(acts)
-    next(acts)
-    next(acts)
-    next(two)
-    next(acts)
-    toks = layer_g(net, g, g_l, bg, lsem.at[2])
-    run([two, acts, toks])
+        steps(f, 2)
+    steps(one, 1)
+    for f in tokens:
+        steps(f, 2)
+    steps(one, 1)
+    run(tokens)
+    fetch = pltpu.make_async_copy(xf, xv, lsem.at[1])
+    fetch.start()
+    steps(two, 1)
+    steps(one, 2)
+    steps(two, 2)
+    toks = layer_g(net, g, g_l, bl, lsem.at[2])
+    steps(toks, 1)
+    steps(one, 2)
+    steps(two, 1)
+    steps(one, 2)
+    steps(two, 1)
+    steps(toks, 1)
+    steps(one, 2)
+    run([two])
+    three = gather_w2(net, w2s, w2f, lsem.at[3])
+    steps(three, 1)
+    run([one])
+    fetch.wait()
+    acts = []
+    for c in range(2):
+        up_tiles(4 * c, w1f, xv, wbuf, uv, av, wsem)
+        keep_a = pltpu.make_async_copy(av.at[:, chunks[c]], act.at[:, chunks[c]], lsem.at[0])
+        keep_u = pltpu.make_async_copy(uv.at[:, chunks[c]], pre.at[:, chunks[c]], lsem.at[1])
+        keep_a.start()
+        keep_u.start()
+        keep_a.wait()
+        acts.append(move_act(net, act, act_l, chunks[c], mids.at[c], txa.at[c], tya.at[c], lsem.at[4 + c]))
+        steps(acts[c], 1)
+        keep_u.wait()
+    for n in (1, 2):
+        steps(acts[0], n)
+        steps(acts[1], n)
+    steps(three, 1)
+    for f in acts:
+        steps(f, 1)
+    steps(three, 1)
+    for f in acts:
+        steps(f, 2)
+    run([three] + acts + [toks])
     net.finish()
 
 
@@ -396,13 +477,20 @@
     net.finish()
 
 
-def fourth_gather(d_pre, dxs, d_pre_l, dxb, bd, ty, lsem, ssem, rsem):
+def fourth_gather(d_pre, dxs, part, d_pre_l, dxb, part_b, bd, ty, tz, lsem, ssem, rsem):
     net = Net(ssem, rsem)
+    ups = exchange_layers(net, part, part_b, tz)
+    steps(ups, 1)
     sums = exchange_sums(net, dxs, dxb, ty)
-    next(sums)
+    steps(sums, 1)
     dp = gather_dpre(net, d_pre, 1, d_pre_l, bd, lsem.at[0])
-    run([dp, sums])
+    run([dp, ups, sums])
     net.finish()
+
+
+def blocks(a, order):
+    size = a.shape[1] // len(order)
+    return jnp.concatenate([a[:, b * size:(b + 1) * size] for b in order], axis=1)
 
 
 def comm(body, outs, bufs, n_local, n_remote, *args):
@@ -413,7 +501,7 @@
         in_specs=[hbm] * len(args),
         out_specs=[hbm] * len(outs),
         scratch_shapes=[pltpu.VMEM(s, d) for s, d in bufs] + [
-            pltpu.SemaphoreType.DMA((n_local,)), pltpu.SemaphoreType.DMA((n_remote,)), pltpu.SemaphoreType.DMA((n_remote,))],
+            pltpu.SemaphoreType.DMA((n,)) for n in (*n_local, n_remote, n_remote)],
         compiler_params=pltpu.CompilerParams(has_side_effects=True),
         cost_estimate=pl.CostEstimate(flops=80_000_000_000, bytes_accessed=64 << 20, transcendentals=0),
     )(*args)
@@ -438,20 +526,15 @@
         k = lax.rem(lax.axis_index("row"), 2)
         y = lax.axis_index("col")
 
-        w1f, w2s, xf, gf = comm(
-            first_gather,
-            [((2 * NX * hr, fk), bf16), ((fk // 8, hid), bf16), ((tok, hid), bf16), ((tok, hid), bf16)],
+        w1f, w2f, xf, gf, pre_act, act, act_l, g_l = comm(
+            first_kernel,
+            [((2 * NX * hr, fk), bf16), ((fk, hid), bf16), ((tok, hid), bf16), ((tok, hid), bf16), ((tok, fk), f32), ((tok, fk), bf16),
+             ((NX, 4, tok // 4, fk), bf16), ((2 * NX, tb, hb), bf16)],
             [((hr, fk), bf16), ((4, fk // 8, hb), bf16), ((2, fk // 16, hb), bf16), ((2, fk // 16, hb), bf16),
-             ((tb, hb), bf16), ((tb, hb), bf16)], 4, 80,
+             ((tb, hb), bf16), ((tb, hb), bf16), ((tb, hb), bf16), ((fk // 8, hid), bf16), ((tok, hid), bf16), ((2, hid, fk // 8), bf16),
+             ((tok, fk), f32), ((tok, fk), bf16), ((2, 4, tok // 4, fk // 2), bf16), ((2, 2, tok // 8, fk // 2), bf16),
+             ((2, 2, tok // 8, fk // 2), bf16)], (6, 2), 160,
             w_up, w_down, x_loc, g_loc)
-        pre_act = dot(xf, w1f, ((1,), (0,)))
-        act = gelu_fwd(pre_act).astype(bf16)
-        w2f, act_l, g_l = comm(
-            second_gather,
-            [((fk, hid), bf16), ((NX, 4, tok // 4, fk), bf16), ((2 * NX, tb, hb), bf16)],
-            [((fk // 8, hid), bf16), ((4, tok // 4, fk), bf16), ((2, tok // 8, fk), bf16), ((2, tok // 8, fk), bf16),
-             ((tb, hb), bf16)], 3, 80,
-            w2s, act, g_loc)
         d_act = dot(gf, w2f, ((1,), (1,)))
         d_pre = (d_act * gelu_slope(pre_act)).astype(bf16)
         dw_down_part = dot(act_l.reshape(NX * tok, fk), g_l.reshape(NX * tok, hb), ((0,), (0,)))
@@ -470,29 +553,31 @@
         d_pre_l0, x_l, yb = comm(
             third_gather,
             [((NX, tok, fk // 2), bf16), ((2 * NX, tb, hb), bf16), ((3, tb, hb), f32)],
-            [((tok, fk // 2), bf16), ((tb, hb), bf16), ((2, tb // 2, hb), bf16), ((2, tb // 2, hb), f32)], 2, 64,
+            [((tok, fk // 2), bf16), ((tb, hb), bf16), ((2, tb // 2, hb), bf16), ((2, tb // 2, hb), f32)], (2,), 64,
             d_pre, xf, ys)
-        x_l = x_l.reshape(NX * tok, 2, NZ, hr // NZ).transpose(0, 2, 1, 3).reshape(NX * tok, hb)
+        x_l = x_l.reshape(NX * tok, hb)
 
         def up_part(d_pre_l):
             return dot(x_l, d_pre_l.reshape(NX * tok, fk // 2), ((0,), (0,)))
 
         part0 = up_part(d_pre_l0)
         dxs = core_sum(dot(d_pre, w1f, ((1,), (1,))))
-        d_pre, part0 = lax.optimization_barrier((d_pre, part0))
-        d_pre_l1, dxb = comm(
+        d_pre_l1, dxb, part_b = comm(
             fourth_gather,
-            [((NX, tok, fk // 2), bf16), ((3, tb, hb), f32)],
-            [((tok, fk // 2), bf16), ((2, tb // 2, hb), f32)], 1, 40,
-            d_pre, dxs)
-        part0, dw_down = lax.optimization_barrier((part0, dw_down))
+            [((NX, tok, fk // 2), bf16), ((3, tb, hb), f32), ((3, 2 * hr // NZ, fk // 2), f32)],
+            [((tok, fk // 2), bf16), ((2, tb // 2, hb), f32), ((2, hr // NZ, fk // 2), f32)], (1,), 40,
+            d_pre, dxs, part0)
+        own = lax.dynamic_slice_in_dim(part0, lax.axis_index("dep") * (2 * hr // NZ), 2 * hr // NZ, 0)
+        totals = [own + part_b[0] + part_b[1] + part_b[2],
+                  lax.psum_scatter(up_part(d_pre_l1), "dep", scatter_dimension=0, tiled=True)]
         outs = []
-        for part in (part0, up_part(d_pre_l1)):
-            total = lax.psum_scatter(part, "dep", scatter_dimension=0, tiled=True).reshape(2, hr // NZ, fk // 2)
+        for total in totals:
+            total = total.reshape(2, hr // NZ, fk // 2)
             keep = jnp.where(k == 0, total[0], total[1])
             take = lax.ppermute(jnp.where(k == 0, total[1], total[0]), "row", swap)
             outs.append((jnp.where(k == 0, keep, take), jnp.where(k == 0, take, keep)))
         dw_up = jnp.concatenate([outs[0][0], outs[1][0], outs[0][1], outs[1][1]], axis=1)
-        return col_sum(ys, yb), col_sum(dxs, dxb), dw_up, dw_down
+        natural = [2 * q + c for c in range(2) for q in range(NZ)]
+        return col_sum(ys, yb), blocks(col_sum(dxs, dxb), natural), dw_up, dw_down
 
     return jax.shard_map(local_block, mesh=mesh, in_specs=(act_spec, wgt_spec, wgt_spec, act_spec), out_specs=(act_spec, act_spec, grad_spec, grad_spec), check_vma=False)

time: 655 us -> 663 us (1.012)
  waiting for transfers between devices: 91 us -> 116 us
  local copies, waits for them, and re-layouts: 24.7 us -> 9.47 us
  matrix products: 91.9 us -> 78 us
  Pallas kernels: 402 us -> 411 us
    reduce_scatter x1, waiting for transfers between devices: 0.02 us -> 76 us  [local_block(): lax.psum_scatter(dw_down_part, 'dep', scatter_dimension=0, tiled=True)]
    reduce_scatter x2 -> x1, waiting for transfers between devices: 90.2 us -> 39.7 us  [local_block(): lax.psum_scatter(up_part(d_pre_l1), 'dep', scatter_dimension=0, tiled=True)]
    reshape x2 -> x0, local copies, waits for them, and re-layouts: 15.2 us -> none  [local_block(): x_l.reshape(NX * tok, 2, NZ, hr // NZ).transpose(0, 2, 1, 3)]
    dot_general x7 -> x6, matrix products: 91.9 us -> 78 us  [dot(): return lax.dot_general(a, b, (dims, ((), ())), preferred_element_type=f32)]
    pallas_call x4 -> x3, Pallas kernels: 402 us -> 411 us  [comm(): pl.pallas_call(body, out_shape=[jax.ShapeDtypeStruct(s, d) for s, d in ou...]
  transfers between devices with their start and end apart: 7 -> 6, of which waited for: 2 -> 2; matrix products, arithmetic and copies ran while one was open for 16% -> 11% of each run, Pallas kernels for 19% -> 10%
where the time goes in v3:
time: 663 us; the launch traced here: 662 us
  Pallas kernels  411 us (62%)
  waiting for transfers between devices  116 us (17%)
  matrix products  78 us (12%)
  other arithmetic  22.3 us (3%)
  between operations  14.2 us (2%)
  starting transfers between devices  10.7 us (2%)
  local copies, waits for them, and re-layouts  9.47 us (1%)
    pallas_call x3, Pallas kernels, comm(): pl.pallas_call(body, out_shape=[jax.ShapeDtypeStruct(s, d) for s, d in ou...  411 us
    dot_general x6, matrix products, dot(): return lax.dot_general(a, b, (dims, ((), ())), preferred_element_type=f32)  78 us
    reduce_scatter x1, waiting for transfers between devices, local_block(): lax.psum_scatter(dw_down_part, 'dep', scatter_dimension=0, tiled=True)  76 us
    reduce_scatter x1, waiting for transfers between devices, local_block(): lax.psum_scatter(up_part(d_pre_l1), 'dep', scatter_dimension=0, tiled=True)  39.7 us
  transfers between devices with their start and end apart: 6, of which 2 were waited for; matrix products, arithmetic and copies ran while one was open for 11% of the time, Pallas kernels for 10%

profile of v3, /device:TPU:1, one launch (start us, length us, event | category | flops | bytes accessed | tf_op | source)
XLA Modules:
  0.0 662.1 jit_solution(8651918318945427982)
XLA Ops:
  7.2 286.1 %shard_map.75 = (bf16[4096,2048]{1,0:T(8,128)(2,1)}, bf16[2048,4096]{1,0:T(8,128)(2,1)}, bf16[512,4096]{1,0:T(8,128)(2,1)}, bf16[512,4096]{1,0:T(8,128)(2,1)}, f...) custom-call(bf16[512,4096]{1,0:T(8,128)(2,1)} %w1.1, ...), custom_call_target="tpu_custom_call" | custom-call | flops 80000000000 | bytes 67108864 | tf_op jit(solution)/shard_map/pallas_call | solution.py:498
  293.3 14.9 %fusion.9 = f32[512,4096]{1,0:T(8,128)} fusion(bf16[512,2048]{1,0:T(8,128)(2,1)} %get-tuple-element.19, bf16[2048,4096]{1,0:T(8,128)(2,1)} %get-tuple-element.20), kind=kOutput, calls=%fused_computation.41 | convolution fusion | flops 8589934592 | bytes 27262976 | tf_op jit(solution)/shard_map/dot_general | solution.py:518
  308.3 4.7 constant_dynamic-slice_fusion.1
  313.0 8.6 %collective-permute-start = (f32[256,4096]{1,0:T(8,128)}, f32[256,4096]{1,0:T(8,128)}, u32[]{:S(2)}, u32[]{:S(2)}) collective-permute-start(f32[256,4096]{1,0:T(8,128)} %constant_dynamic-slice_fusion.1), channel_id=1, source_target_pairs={{0,1},{1,0},{2,3},{3,2},{4,5},{5,4},{6,7},{7,6},{8,9},{9,8},{10,11... | collective-permute-start | bytes 12582920 | tf_op jit(solution)/shard_map/ppermute | solution.py:546
  321.6 17.2 %fusion.6.d_pre = bf16[512,2048]{1,0:T(8,128)(2,1)} fusion(f32[512,2048]{1,0:T(8,128)} %get-tuple-element.22, bf16[512,4096]{1,0:T(8,128)(2,1)} %get-tuple-element.21, bf16[2048,4096]{1,0:T(8,128)(2,1)} %get-tuple-element.20), kind=kOutput, calls=%fused_computation.8 | convolution fusion | flops 8609857536 | bytes 27262976 | tf_op jit(solution)/shard_map/dot_general | solution.py:518
  338.9 13.3 %fusion.10 = f32[2048,1024]{1,0:T(8,128)} fusion(bf16[2048,2048]{1,0:T(8,128)(2,1)S(1)} %bitcast.53, bf16[2048,1024]{1,0:T(8,128)(2,1)} %bitcast.54), kind=kOutput, calls=%fused_computation.42 | convolution fusion | flops 8589934592 | bytes 20971520 | tf_op jit(solution)/shard_map/dot_general | solution.py:518
  352.2 12.4 %fusion.11 = f32[512,4096]{1,0:T(8,128)S(1)} fusion(bf16[512,2048]{1,0:T(8,128)(2,1)} %fusion.6.d_pre, bf16[4096,2048]{1,0:T(8,128)(2,1)} %get-tuple-element.28), kind=kOutput, calls=%fused_computation.43 | convolution fusion | flops 8589934592 | bytes 27262976 | tf_op jit(solution)/shard_map/dot_general | solution.py:518
  364.6 2.5 constant_dynamic-slice_fusion
  367.0 2.0 copy-done
  369.0 6.1 dynamic-slice_add_fusion.1.ys
  375.1 67.4 %shard_map.76 = (bf16[4,512,1024]{2,1,0:T(8,128)(2,1)}, bf16[8,256,1024]{2,1,0:T(8,128)(2,1)}, f32[3,256,1024]{2,1,0:T(8,128)}) custom-call(bf16[512,2048]{1,0:T(8,128)(2,1)} %fusion.6.d_pre, bf16[512,4096]{1,0:T(8,128)(2,1)} %get-tuple-element.26.xf, f32[256,4096]{1,0:T(8,128)} %dynamic-slice_add_fusion.1.ys), custom_call_target="tpu_custom_call" | custom-call | flops 80000000000 | bytes 67108864 | tf_op jit(solution)/shard_map/pallas_call | solution.py:498
  442.6 10.2 %fusion.12.part = f32[1024,1024]{1,0:T(8,128)} fusion(bf16[2048,1024]{1,0:T(8,128)(2,1)} %bitcast.55, bf16[2048,1024]{1,0:T(8,128)(2,1)} %bitcast.58), kind=kOutput, calls=%fused_computation.44 | convolution fusion | flops 4294967296 | bytes 12582912 | tf_op jit(solution)/shard_map/dot_general | solution.py:518
  452.8 4.7 dynamic-slice_add_fusion.dxs
  457.6 57.4 %shard_map.77 = (bf16[4,512,1024]{2,1,0:T(8,128)(2,1)}, f32[3,256,1024]{2,1,0:T(8,128)}, f32[3,256,1024]{2,1,0:T(8,128)}) custom-call(bf16[512,2048]{1,0:T(8,128)(2,1)} %fusion.6.d_pre, f32[256,4096]{1,0:T(8,128)} %dynamic-slice_add_fusion.dxs, f32[1024,1024]{1,0:T(8,128)} %fusion.12.part), custom_call_target="tpu_custom_call" | custom-call | flops 80000000000 | bytes 67108864 | tf_op jit(solution)/shard_map/pallas_call | solution.py:498
  515.0 10.0 %fusion.13 = f32[1024,1024]{1,0:T(8,128)} fusion(bf16[2048,1024]{1,0:T(8,128)(2,1)} %bitcast.56, bf16[2048,1024]{1,0:T(8,128)(2,1)} %bitcast.57), kind=kOutput, calls=%fused_computation.45 | convolution fusion | flops 4294967296 | bytes 12582912 | tf_op jit(solution)/shard_map/dot_general | solution.py:518
  525.8 2.6 bitcast_add_fusion
  528.4 0.9 collective-permute-start.2
  529.4 2.5 fusion.7
  532.2 39.7 %reduce-scatter.3.cloned.1.call-done = f32[256,1024]{1,0:T(8,128)} async-done(((f32[1024,1024]{1,0:T(8,128)}), f32[256,1024]{1,0:T(8,128)}) %reduce-scatter.3.cloned.1.call-update) | async-done | bytes 1048592 | tf_op jit(solution)/shard_map/reduce_scatter | solution.py:572
  571.8 1.3 slice_select_fusion
  573.2 1.0 collective-permute-start.3
  574.2 3.3 fusion.8
  577.8 1.5 pad_maximum_fusion
  579.3 76.0 %reduce-scatter.5.cloned.1.call-done = f32[512,1024]{1,0:T(8,128)} async-done(((f32[2048,1024]{1,0:T(8,128)}), f32[512,1024]{1,0:T(8,128)}) %reduce-scatter.5.cloned.1.call-update) | async-done | bytes 2097168 | tf_op jit(solution)/shard_map/reduce_scatter | solution.py:541
  (32 shorter events, 1.4 us)
Async XLA Ops:
  7.2 564.7 %reduce-scatter.3.cloned.1.call-start = ((), (), s32[]{:S(2)}) async-start(), calls=%async_computation.2 | async-start | bytes 5242880 | tf_op jit(solution)/shard_map/reduce_scatter | solution.py:572
  308.3 30.6 %slice-start = ((s8[8388608]{0:T(1024)(128)(4,1)}), s8[4194304]{0:T(1024)(128)(4,1)S(1)}, s32[]{:S(2)}) async-start(s8[8388608]{0:T(1024)(128)(4,1)} %bitcast.51), calls=%async_computation.4 | async-start | bytes 8388608
  313.0 56.0 %collective-permute-start = (f32[256,4096]{1,0:T(8,128)}, f32[256,4096]{1,0:T(8,128)}, u32[]{:S(2)}, u32[]{:S(2)}) collective-permute-start(f32[256,4096]{1,0:T(8,128)} %constant_dynamic-slice_fusion.1), channel_id=1, source_target_pairs={{0,1},{1,0},{2,3},{3,2},{4,5},{5,4},{6,7},{7,6},{8,9},{9,8},{10,11... | collective-permute-start | bytes 12582920 | tf_op jit(solution)/shard_map/ppermute | solution.py:546
  321.6 17.2 %slice-start.1 = ((s8[8388608]{0:T(1024)(128)(4,1)}), s8[4194304]{0:T(1024)(128)(4,1)S(1)}, s32[]{:S(2)}) async-start(s8[8388608]{0:T(1024)(128)(4,1)} %bitcast.51), calls=%async_computation.5 | async-start | bytes 8388608
  364.5 4.5 copy-start
  369.0 83.8 %collective-permute-start.1 = (f32[256,4096]{1,0:T(8,128)}, f32[256,4096]{1,0:T(8,128)}, u32[]{:S(2)}, u32[]{:S(2)}) collective-permute-start(f32[256,4096]{1,0:T(8,128)} %constant_dynamic-slice_fusion), channel_id=1, source_target_pairs={{0,1},{1,0},{2,3},{3,2},{4,5},{5,4},{6,7},{7,6},{8,9},{9,8},{10,11... | collective-permute-start | bytes 12582920 | tf_op jit(solution)/shard_map/ppermute | solution.py:546
  442.6 10.2 %copy-start.1 = (f32[512,4096]{1,0:T(8,128)S(1)}, f32[512,4096]{1,0:T(8,128)}, u32[]{:S(2)}) copy-start(f32[512,4096]{1,0:T(8,128)} %copy-done) | copy-start | bytes 25165828
  525.0 130.2 %reduce-scatter.5.cloned.1.call-start = ((), (), s32[]{:S(2)}) async-start(), calls=%async_computation.3 | async-start | bytes 10485760 | tf_op jit(solution)/shard_map/reduce_scatter | solution.py:541
  528.4 49.1 %collective-permute-start.2 = (f32[128,1024]{1,0:T(8,128)S(1)}, f32[128,1024]{1,0:T(8,128)S(1)}, u32[]{:S(2)}, u32[]{:S(2)}) collective-permute-start(f32[128,1024]{1,0:T(8,128)S(1)} %slice_select_fusion.2), channel_id=1, source_target_pairs={{0,1},{1,0},{2,3},{3,2},{4,5},{5,4},{6,7},{7,6},{8,9},{9,8},{10,11... | collective-permute-start | bytes 1572872 | tf_op jit(solution)/shard_map/ppermute | solution.py:577
  532.2 45.5 %copy-start.3 = (bf16[256,1024]{1,0:T(8,128)(2,1)}, bf16[256,1024]{1,0:T(8,128)(2,1)S(1)}, u32[]{:S(2)}) copy-start(bf16[256,1024]{1,0:T(8,128)(2,1)S(1)} %slice_dynamic-update-slice_fusion) | copy-start | bytes 1572868
  571.8 5.8 copy-start.2
  573.2 4.5 collective-permute-start.3
Sparse Core Ops, SparseCore 0:
  525.1 46.6 reduce-scatter.2
  574.9 80.3 reduce-scatter.4

commit v4 on v3

--- a/solution.py
+++ b/solution.py
@@ -10,6 +10,9 @@
 NX = 4
 NY = 4
 NZ = 4
+FIRST_ORDER = (0, 2, 3, 1, 6, 8, 4, 2, 3, 3, 2, 2, 3, 3, 3, 2, 6, 2, 2, 2, 6, 5, 5, 3, 8, 5, 5, 5, 5, 3, 2, 4, 0, 4, 0, 1, 8, 4, 0, 0, 1, 0, 1, 0, 8, 1, 0, 1, 6, 3, 3, 7, 1, 6, 1, 0, 0, 3, 3, 3, 1, 7, 7, 1, 7, 7, 0, 3, 1)
+THIRD_ORDER = (1, 2, 0, 1, 0, 1, 2, 1, 2, 0, 0, 0, 2, 1, 1, 1)
+FOURTH_ORDER = (0, 1, 2, 0, 1, 2, 2, 1, 2, 0, 2, 2, 2, 0, 1)
 
 
 def gelu_fwd(pre_act):
@@ -73,30 +76,42 @@
         return {"row": 2 * self.x + 1 - self.k}
 
 
+class Gate:
+    opened = False
+
+
+def need(*gates):
+    assert all(gate.opened for gate in gates)
+
+
 def ring(net, place, n, up, down, own, view, arrived, pieces=2):
     west, east, far = rot(place, -1, n), rot(place, 1, n), rot(place, 2, n)
     ups, downs, relays = [], [], []
-    for q in range(pieces):
-        if q == pieces // 2:
-            yield
+
+    def give(q):
         r = pieces - 1 - q
         ups.append(net.send(own(q), view(place, q), up))
         downs.append(net.send(own(r), view(place, r), down))
+
+    give(0)
+    give(1)
     for q in range(pieces):
-        yield
+        yield [ups[q], downs[q]]
         r = pieces - 1 - q
         ups[q].wait_recv()
+        downs[q].wait_recv()
         if q < pieces // 2:
             relays.append((q, net.send(view(west, q), view(west, q), up)))
+            relays.append((r, net.send(view(east, r), view(east, r), down)))
+        if q + 2 < pieces:
+            give(q + 2)
         arrived(west, q)
-        downs[q].wait_recv()
-        if q < pieces // 2:
-            relays.append((r, net.send(view(east, r), view(east, r), down)))
         arrived(east, r)
-    for q, copy in relays:
-        yield
-        copy.wait_recv()
-        arrived(far, q)
+    for n in range(0, len(relays), 2):
+        yield [copy for _, copy in relays[n:n + 2]]
+        for q, copy in relays[n:n + 2]:
+            copy.wait_recv()
+            arrived(far, q)
 
 
 def exchange(net, place, n, up, down, piece, slot, tmp, arrived=lambda j: None):
@@ -105,17 +120,17 @@
     hi = net.send(piece(far, 1), tmp.at[1], down)
     e = net.send(piece(east, None), slot(place, 0, None), up)
     w = net.send(piece(west, None), slot(place, 1, None), down)
-    yield
+    yield [lo, hi]
     lo.wait_recv()
     lo = net.send(tmp.at[0], slot(west, 2, 0), up)
     hi.wait_recv()
     hi = net.send(tmp.at[1], slot(east, 2, 1), down)
-    yield
+    yield [e, w]
     e.wait_recv()
     arrived(west)
     w.wait_recv()
     arrived(east)
-    yield
+    yield [lo, hi]
     lo.wait_recv()
     hi.wait_recv()
     arrived(far)
@@ -144,7 +159,7 @@
     load = pltpu.make_async_copy(w1.at[:, mine], buf, sem)
     load.start()
     swaps = [net.send(w1.at[pl.ds(q * size, size), other], slot(net.x, q, net.k), net.partner()) for q in range(4)]
-    yield
+    yield swaps
     load.wait()
     stores = [pltpu.make_async_copy(buf.at[pl.ds(q * size, size), :], slot(net.x, q, net.k), sem) for q in range(4)]
     for copy in stores:
@@ -159,7 +174,7 @@
 
     got = []
     yield from ring(net, net.x, NX, net.at_x(1), net.at_x(-1), lambda q: view(net.x, q), view, to_z(net, view, got, 4), 4)
-    yield
+    yield got
     for copy in got:
         copy.wait_recv()
 
@@ -188,11 +203,12 @@
         passed.append(net.send(view(j, h), view(j, h), net.partner()))
 
     gather = ring(net, net.y, NY, net.at_y(1), net.at_y(-1), lambda h: src.at[rows_of(0, rows, h), :], view, arrived)
-    next(gather)
+    first = next(gather)
     store = pltpu.make_async_copy(buf, view(net.y, None), sem)
     store.start()
+    yield first
     yield from gather
-    yield
+    yield passed
     store.wait()
     for copy in passed:
         copy.wait_recv()
@@ -233,17 +249,28 @@
 
     got = []
     gather = ring(net, net.x, NX, net.at_x(1), net.at_x(-1), own, view, to_z(net, view, got, 4), 4)
-    next(gather)
-    for q in (0, 3, 1, 2):
-        got.append(net.send(own(q), view(net.x, q), net.at_z(1 if q < 2 else -1)))
+    first = next(gather)
     store = pltpu.make_async_copy(w2s, w2f.at[pl.ds(pl.multiple_of(base + net.x * rows, rows), rows), :], sem)
     store.start()
-    yield
+    yield first
     yield from gather
-    yield
+    yield got
     for copy in got:
         copy.wait_recv()
     store.wait()
+
+
+def layers_w2(net, w2s, w2f):
+    rows = w2s.shape[0]
+    size = rows // 4
+    base = lax.rem(net.z, 2) * 4 * rows + net.x * rows
+    for q in range(2):
+        got = []
+        for p, d in ((q, 1), (3 - q, -1)):
+            got.append(net.send(w2s.at[pl.ds(p * size, size), :], w2f.at[pl.ds(pl.multiple_of(base + p * size, size), size), :], net.at_z(d)))
+        yield got
+        for copy in got:
+            copy.wait_recv()
 
 
 def move_act(net, act, act_l, cs, mid, tx, ty, sem):
@@ -283,12 +310,13 @@
         passed.append(net.send(view(i, h), view(i, h), net.partner()))
 
     gather = ring(net, net.x, NX, net.at_x(1), net.at_x(-1), lambda h: g.at[rows_of(0, rows, h), :], view, arrived)
-    next(gather)
+    first = next(gather)
     load.wait()
     store = pltpu.make_async_copy(buf, view(net.x, None), sem)
     store.start()
+    yield first
     yield from gather
-    yield
+    yield passed
     store.wait()
     for copy in passed:
         copy.wait_recv()
@@ -313,13 +341,13 @@
         passed.append(net.send(slot(j, 0, None), slot(j, 0, None), net.partner()))
 
     moves = exchange(net, net.x, NX, net.at_x(1), net.at_x(-1), piece, slot, tmp, arrived)
-    next(moves)
+    first = next(moves)
     load.wait()
     store = pltpu.make_async_copy(buf, own, sem)
     store.start()
-    yield
+    yield first
     yield from moves
-    yield
+    yield passed
     store.wait()
     for copy in passed:
         copy.wait_recv()
@@ -337,12 +365,11 @@
 
     gather = ring(
         net, net.x, NX, net.at_x(1), net.at_x(-1), lambda q: d_pre.at[pl.ds(q * size, size), cs], view, lambda i, q: None, 4)
-    next(gather)
-    next(gather)
+    first = next(gather)
     load.wait()
     store = pltpu.make_async_copy(buf, d_pre_l.at[net.x], sem)
     store.start()
-    yield
+    yield first
     yield from gather
     store.wait()
 
@@ -367,7 +394,9 @@
         net, net.z, NZ, net.at_z(1), net.at_z(-1), piece, lambda j, side, h: dst.at[side, rows_of(0, rows, h), :], tmp)
 
 
-def run(flows):
+def run(flows, order=()):
+    for n in order:
+        next(flows[n], None)
     flows = list(flows)
     while flows:
         flows = [f for f in flows if next(f, flows) is not flows]
@@ -395,11 +424,6 @@
         u = jnp.dot(xv[...], wbuf[slot], preferred_element_type=jnp.float32)
         uv[:, t] = u
         av[:, t] = gelu_fwd(u).astype(av.dtype)
-
-
-def steps(flow, n):
-    for _ in range(n):
-        next(flow, None)
 
 
 def first_kernel(
@@ -408,83 +432,68 @@
     net = Net(ssem, rsem)
     cols = act.shape[1] // 2
     chunks = [pl.ds(c * cols, cols) for c in range(2)]
-    one = gather_w1(net, w1, w1f, b1, lsem.at[0])
-    steps(one, 1)
-    tokens = [gather_tokens(net, x, xf, bx, lsem.at[1], [c * NZ + q for q in range(NZ) for c in range(2)]), gather_tokens(net, g, gf, bg, lsem.at[2])]
-    for f in tokens:
-        steps(f, 1)
-    steps(one, 2)
-    two = move_w2(net, w2, w2s, mid, tx, ty, lsem.at[3])
-    steps(two, 1)
-    for f in tokens:
-        steps(f, 2)
-    steps(one, 1)
-    for f in tokens:
-        steps(f, 2)
-    steps(one, 1)
-    run(tokens)
-    fetch = pltpu.make_async_copy(xf, xv, lsem.at[1])
-    fetch.start()
-    steps(two, 1)
-    steps(one, 2)
-    steps(two, 2)
-    toks = layer_g(net, g, g_l, bl, lsem.at[2])
-    steps(toks, 1)
-    steps(one, 2)
-    steps(two, 1)
-    steps(one, 2)
-    steps(two, 1)
-    steps(toks, 1)
-    steps(one, 2)
-    run([two])
-    three = gather_w2(net, w2s, w2f, lsem.at[3])
-    steps(three, 1)
-    run([one])
-    fetch.wait()
-    acts = []
-    for c in range(2):
-        up_tiles(4 * c, w1f, xv, wbuf, uv, av, wsem)
-        keep_a = pltpu.make_async_copy(av.at[:, chunks[c]], act.at[:, chunks[c]], lsem.at[0])
-        keep_u = pltpu.make_async_copy(uv.at[:, chunks[c]], pre.at[:, chunks[c]], lsem.at[1])
-        keep_a.start()
-        keep_u.start()
-        keep_a.wait()
-        acts.append(move_act(net, act, act_l, chunks[c], mids.at[c], txa.at[c], tya.at[c], lsem.at[4 + c]))
-        steps(acts[c], 1)
-        keep_u.wait()
-    for n in (1, 2):
-        steps(acts[0], n)
-        steps(acts[1], n)
-    steps(three, 1)
-    for f in acts:
-        steps(f, 1)
-    steps(three, 1)
-    for f in acts:
-        steps(f, 2)
-    run([three] + acts + [toks])
+    w1_here, x_here, a_here, w2_moved = Gate(), Gate(), [Gate(), Gate()], Gate()
+
+    def weights1():
+        yield from gather_w1(net, w1, w1f, b1, lsem.at[0])
+        w1_here.opened = True
+
+    def tokens_x():
+        yield from gather_tokens(net, x, xf, bx, lsem.at[1], [c * NZ + q for q in range(NZ) for c in range(2)])
+        fetch = pltpu.make_async_copy(xf, xv, lsem.at[1])
+        fetch.start()
+        yield []
+        fetch.wait()
+        x_here.opened = True
+
+    def weights2():
+        yield from move_w2(net, w2, w2s, mid, tx, ty, lsem.at[3])
+        w2_moved.opened = True
+        yield from gather_w2(net, w2s, w2f, lsem.at[3])
+
+    def up():
+        yield [w1_here, x_here]
+        need(w1_here, x_here)
+        for c in range(2):
+            up_tiles(4 * c, w1f, xv, wbuf, uv, av, wsem)
+            keep_a = pltpu.make_async_copy(av.at[:, chunks[c]], act.at[:, chunks[c]], lsem.at[6])
+            keep_u = pltpu.make_async_copy(uv.at[:, chunks[c]], pre.at[:, chunks[c]], lsem.at[7])
+            keep_a.start()
+            keep_u.start()
+            keep_a.wait()
+            keep_u.wait()
+            a_here[c].opened = True
+            yield []
+
+    def acts(c):
+        yield [a_here[c]]
+        need(a_here[c])
+        yield from move_act(net, act, act_l, chunks[c], mids.at[c], txa.at[c], tya.at[c], lsem.at[4 + c])
+
+    def weights2_own():
+        yield [w2_moved]
+        need(w2_moved)
+        yield from layers_w2(net, w2s, w2f)
+
+    def layer():
+        yield from layer_g(net, g, g_l, bl, lsem.at[8])
+
+    flows = [acts(0), acts(1), weights1(), weights2(), up(), tokens_x(), gather_tokens(net, g, gf, bg, lsem.at[2]), layer(), weights2_own()]
+    run(flows, FIRST_ORDER)
     net.finish()
 
 
 def third_gather(d_pre, xf, ys, d_pre_l, x_l, yb, bd, bx, tx, ty, lsem, ssem, rsem):
     net = Net(ssem, rsem)
-    sums = exchange_sums(net, ys, yb, ty)
-    next(sums)
-    dp = gather_dpre(net, d_pre, 0, d_pre_l, bd, lsem.at[0])
-    next(dp)
-    toks = layer_x(net, xf, x_l, bx, tx, lsem.at[1])
-    next(toks)
-    run([dp, toks, sums])
+    run([layer_x(net, xf, x_l, bx, tx, lsem.at[1]), gather_dpre(net, d_pre, 0, d_pre_l, bd, lsem.at[0]), exchange_sums(net, ys, yb, ty)],
+        THIRD_ORDER)
     net.finish()
 
 
 def fourth_gather(d_pre, dxs, part, d_pre_l, dxb, part_b, bd, ty, tz, lsem, ssem, rsem):
     net = Net(ssem, rsem)
-    ups = exchange_layers(net, part, part_b, tz)
-    steps(ups, 1)
-    sums = exchange_sums(net, dxs, dxb, ty)
-    steps(sums, 1)
-    dp = gather_dpre(net, d_pre, 1, d_pre_l, bd, lsem.at[0])
-    run([dp, ups, sums])
+    run([exchange_layers(net, part, part_b, tz), exchange_sums(net, dxs, dxb, ty), gather_dpre(net, d_pre, 1, d_pre_l, bd, lsem.at[0])],
+        FOURTH_ORDER)
     net.finish()
 
 
@@ -533,7 +542,7 @@
             [((hr, fk), bf16), ((4, fk // 8, hb), bf16), ((2, fk // 16, hb), bf16), ((2, fk // 16, hb), bf16),
              ((tb, hb), bf16), ((tb, hb), bf16), ((tb, hb), bf16), ((fk // 8, hid), bf16), ((tok, hid), bf16), ((2, hid, fk // 8), bf16),
              ((tok, fk), f32), ((tok, fk), bf16), ((2, 4, tok // 4, fk // 2), bf16), ((2, 2, tok // 8, fk // 2), bf16),
-             ((2, 2, tok // 8, fk // 2), bf16)], (6, 2), 160,
+             ((2, 2, tok // 8, fk // 2), bf16)], (9, 2), 160,
             w_up, w_down, x_loc, g_loc)
         d_act = dot(gf, w2f, ((1,), (1,)))
         d_pre = (d_act * gelu_slope(pre_act)).astype(bf16)
@@ -562,6 +571,7 @@
 
         part0 = up_part(d_pre_l0)
         dxs = core_sum(dot(d_pre, w1f, ((1,), (1,))))
+        part0, dw_down = lax.optimization_barrier((part0, dw_down))
         d_pre_l1, dxb, part_b = comm(
             fourth_gather,
             [((NX, tok, fk // 2), bf16), ((3, tb, hb), f32), ((3, 2 * hr // NZ, fk // 2), f32)],

time: 663 us -> 539 us (0.81)
  waiting for transfers between devices: 116 us -> 39.4 us
  Pallas kernels: 411 us -> 372 us
  starting transfers between devices: 10.7 us -> 3.84 us
    reduce_scatter x1, waiting for transfers between devices: 76 us -> 0.01 us  [local_block(): lax.psum_scatter(dw_down_part, 'dep', scatter_dimension=0, tiled=True)]
    pallas_call x3, Pallas kernels: 411 us -> 372 us  [comm(): pl.pallas_call(body, out_shape=[jax.ShapeDtypeStruct(s, d) for s, d in ou...]
    ppermute x2, starting transfers between devices: 8.62 us -> 1.81 us  [core_sum(): return keep + lax.ppermute(give, 'row', swap)]
  transfers between devices with their start and end apart: 6 -> 6, of which waited for: 2 -> 2; matrix products, arithmetic and copies ran while one was open for 11% -> 14% of each run, Pallas kernels for 10% -> 12%
where the time goes in v4:
time: 539 us; the launch traced here: 538 us
  Pallas kernels  372 us (69%)
  matrix products  76.5 us (14%)
  waiting for transfers between devices  39.4 us (7%)
  other arithmetic  19.7 us (4%)
  between operations  14.2 us (3%)
  local copies, waits for them, and re-layouts  12.9 us (2%)
    pallas_call x3, Pallas kernels, comm(): pl.pallas_call(body, out_shape=[jax.ShapeDtypeStruct(s, d) for s, d in ou...  372 us
    dot_general x6, matrix products, dot(): return lax.dot_general(a, b, (dims, ((), ())), preferred_element_type=f32)  76.5 us
    reduce_scatter x1, waiting for transfers between devices, local_block(): lax.psum_scatter(up_part(d_pre_l1), 'dep', scatter_dimension=0, tiled=True)  38 us
    add x2, other arithmetic, core_sum(): return keep + lax.ppermute(give, 'row', swap)  10.8 us
  transfers between devices with their start and end apart: 6, of which 2 were waited for; matrix products, arithmetic and copies ran while one was open for 14% of the time, Pallas kernels for 12%

profile of v4, /device:TPU:1, one launch (start us, length us, event | category | flops | bytes accessed | tf_op | source)
XLA Modules:
  0.0 538.1 jit_solution(3562931517178040693)
XLA Ops:
  7.2 247.8 %shard_map.75 = (bf16[4096,2048]{1,0:T(8,128)(2,1)}, bf16[2048,4096]{1,0:T(8,128)(2,1)}, bf16[512,4096]{1,0:T(8,128)(2,1)}, bf16[512,4096]{1,0:T(8,128)(2,1)}, f...) custom-call(bf16[512,4096]{1,0:T(8,128)(2,1)} %w1.1, ...), custom_call_target="tpu_custom_call" | custom-call | flops 80000000000 | bytes 67108864 | tf_op jit(solution)/shard_map/pallas_call | solution.py:507
  255.0 14.6 %fusion.10 = f32[2048,1024]{1,0:T(8,128)} fusion(bf16[2048,2048]{1,0:T(8,128)(2,1)} %bitcast.51, bf16[2048,1024]{1,0:T(8,128)(2,1)} %bitcast.54), kind=kOutput, calls=%fused_computation.42 | convolution fusion | flops 8589934592 | bytes 20971520 | tf_op jit(solution)/shard_map/dot_general | solution.py:527
  269.7 1.5 copy-done.8
  271.2 14.4 %fusion.9 = f32[512,4096]{1,0:T(8,128)} fusion(bf16[512,2048]{1,0:T(8,128)(2,1)S(1)} %copy-done.8, bf16[2048,4096]{1,0:T(8,128)(2,1)} %get-tuple-element.22), kind=kOutput, calls=%fused_computation.41 | convolution fusion | flops 8589934592 | bytes 27262976 | tf_op jit(solution)/shard_map/dot_general | solution.py:527
  285.6 4.8 constant_dynamic-slice_fusion.1
  290.3 1.8 collective-permute-start
  292.1 14.9 %fusion.6.d_pre = bf16[512,2048]{1,0:T(8,128)(2,1)S(1)} fusion(f32[512,2048]{1,0:T(8,128)} %get-tuple-element.24, bf16[512,4096]{1,0:T(8,128)(2,1)S(1)} %copy-done.9, bf16[2048,4096]{1,0:T(8,128)(2,1)} %get-tuple-element.22), kind=kOutput, calls=%fused_computation.8 | convolution fusion | flops 8609857536 | bytes 27262976 | tf_op jit(solution)/shard_map/dot_general | solution.py:527
  307.1 12.5 %fusion.11 = f32[512,4096]{1,0:T(8,128)S(1)} fusion(bf16[512,2048]{1,0:T(8,128)(2,1)S(1)} %fusion.6.d_pre, bf16[4096,2048]{1,0:T(8,128)(2,1)} %get-tuple-element.30), kind=kOutput, calls=%fused_computation.43 | convolution fusion | flops 8589934592 | bytes 27262976 | tf_op jit(solution)/shard_map/dot_general | solution.py:527
  319.6 2.5 constant_dynamic-slice_fusion
  322.0 2.1 copy-done
  324.1 6.1 %dynamic-slice_add_fusion.1.ys = f32[256,4096]{1,0:T(8,128)} fusion(f32[256,4096]{1,0:T(8,128)} %collective-permute-done, f32[512,4096]{1,0:T(8,128)} %fusion.9, s32[]{:T(128)S(6)} %select_n.51), kind=kLoop, calls=%fused_computation.10 | loop fusion | flops 1048576 | bytes 12582916 | tf_op jit(solution)/shard_map/add | solution.py:555
  330.2 66.4 %shard_map.76 = (bf16[4,512,1024]{2,1,0:T(8,128)(2,1)}, bf16[8,256,1024]{2,1,0:T(8,128)(2,1)}, f32[3,256,1024]{2,1,0:T(8,128)}) custom-call(bf16[512,2048]{1,0:T(8,128)(2,1)} %copy-done.7, bf16[512,4096]{1,0:T(8,128)(2,1)} %get-tuple-element.28.xf, f32[256,4096]{1,0:T(8,128)} %dynamic-slice_add_fusion.1.ys), custom_call_target="tpu_custom_call" | custom-call | flops 80000000000 | bytes 67108864 | tf_op jit(solution)/shard_map/pallas_call | solution.py:507
  396.6 10.1 %fusion.12.part = f32[1024,1024]{1,0:T(8,128)} fusion(bf16[2048,1024]{1,0:T(8,128)(2,1)} %bitcast.52, bf16[2048,1024]{1,0:T(8,128)(2,1)} %bitcast.56), kind=kOutput, calls=%fused_computation.44 | convolution fusion | flops 4294967296 | bytes 12582912 | tf_op jit(solution)/shard_map/dot_general | solution.py:527
  406.7 4.7 dynamic-slice_add_fusion.dxs
  411.4 57.4 %shard_map.77 = (bf16[4,512,1024]{2,1,0:T(8,128)(2,1)}, f32[3,256,1024]{2,1,0:T(8,128)}, f32[3,256,1024]{2,1,0:T(8,128)}) custom-call(bf16[512,2048]{1,0:T(8,128)(2,1)} %copy-done.7, f32[256,4096]{1,0:T(8,128)} %dynamic-slice_add_fusion.dxs, f32[1024,1024]{1,0:T(8,128)} %fusion.12.part), custom_call_target="tpu_custom_call" | custom-call | flops 80000000000 | bytes 67108864 | tf_op jit(solution)/shard_map/pallas_call | solution.py:507
  468.8 10.0 %fusion.13 = f32[1024,1024]{1,0:T(8,128)} fusion(bf16[2048,1024]{1,0:T(8,128)(2,1)} %bitcast.53, bf16[2048,1024]{1,0:T(8,128)(2,1)} %bitcast.55), kind=kOutput, calls=%fused_computation.45 | convolution fusion | flops 4294967296 | bytes 12582912 | tf_op jit(solution)/shard_map/dot_general | solution.py:527
  478.9 1.8 copy-done.3
  480.7 2.4 fusion.8
  483.1 1.8 bitcast_add_fusion
  485.9 1.6 fusion.7
  487.7 38.0 %reduce-scatter.5.cloned.1.call-done = f32[256,1024]{1,0:T(8,128)} async-done(((f32[1024,1024]{1,0:T(8,128)}), f32[256,1024]{1,0:T(8,128)}) %reduce-scatter.5.cloned.1.call-update) | async-done | bytes 1048592 | tf_op jit(solution)/shard_map/reduce_scatter | solution.py:582
  525.7 1.3 slice_select_fusion
  528.3 1.3 collective-permute-done.3
  529.8 1.5 pad_maximum_fusion
  (39 shorter events, 2.7 us)
Async XLA Ops:
  7.2 404.2 %reduce-scatter.3.cloned.1.call-start = ((), (), s32[]{:S(2)}) async-start(), calls=%async_computation.2 | async-start | bytes 10485760 | tf_op jit(solution)/shard_map/reduce_scatter | solution.py:550
  269.6 1.6 copy-start.8
  269.6 256.1 %reduce-scatter.5.cloned.1.call-start = ((), (), s32[]{:S(2)}) async-start(), calls=%async_computation.3 | async-start | bytes 5242880 | tf_op jit(solution)/shard_map/reduce_scatter | solution.py:582
  285.6 6.6 %copy-start.9 = (bf16[512,4096]{1,0:T(8,128)(2,1)S(1)}, bf16[512,4096]{1,0:T(8,128)(2,1)}, u32[]{:S(2)}) copy-start(bf16[512,4096]{1,0:T(8,128)(2,1)} %get-tuple-element.23) | copy-start | bytes 12582916
  290.3 33.8 %collective-permute-start = (f32[256,4096]{1,0:T(8,128)}, f32[256,4096]{1,0:T(8,128)}, u32[]{:S(2)}, u32[]{:S(2)}) collective-permute-start(f32[256,4096]{1,0:T(8,128)} %constant_dynamic-slice_fusion.1), channel_id=1, source_target_pairs={{0,1},{1,0},{2,3},{3,2},{4,5},{5,4},{6,7},{7,6},{8,9},{9,8},{10,11... | collective-permute-start | bytes 12582920 | tf_op jit(solution)/shard_map/ppermute | solution.py:555
  307.1 12.5 %copy-start.7 = (bf16[512,2048]{1,0:T(8,128)(2,1)}, bf16[512,2048]{1,0:T(8,128)(2,1)S(1)}, u32[]{:S(2)}) copy-start(bf16[512,2048]{1,0:T(8,128)(2,1)S(1)} %fusion.6.d_pre) | copy-start | bytes 6291460
  319.6 4.5 copy-start
  324.1 82.6 %collective-permute-start.1 = (f32[256,4096]{1,0:T(8,128)}, f32[256,4096]{1,0:T(8,128)}, u32[]{:S(2)}, u32[]{:S(2)}) collective-permute-start(f32[256,4096]{1,0:T(8,128)} %constant_dynamic-slice_fusion), channel_id=1, source_target_pairs={{0,1},{1,0},{2,3},{3,2},{4,5},{5,4},{6,7},{7,6},{8,9},{9,8},{10,11... | collective-permute-start | bytes 12582920 | tf_op jit(solution)/shard_map/ppermute | solution.py:555
  396.6 10.1 %copy-start.1 = (f32[512,4096]{1,0:T(8,128)S(1)}, f32[512,4096]{1,0:T(8,128)}, u32[]{:S(2)}) copy-start(f32[512,4096]{1,0:T(8,128)} %copy-done) | copy-start | bytes 25165828
  478.9 1.9 copy-start.3
  478.9 4.2 copy-start.5
  483.1 2.8 copy-start.4
  485.0 43.2 %collective-permute-start.2 = (f32[128,1024]{1,0:T(8,128)S(1)}, f32[128,1024]{1,0:T(8,128)S(1)}, u32[]{:S(2)}, u32[]{:S(2)}) collective-permute-start(f32[128,1024]{1,0:T(8,128)S(1)} %slice_select_fusion.2), channel_id=1, source_target_pairs={{0,1},{1,0},{2,3},{3,2},{4,5},{5,4},{6,7},{7,6},{8,9},{9,8},{10,11... | collective-permute-start | bytes 1572872 | tf_op jit(solution)/shard_map/ppermute | solution.py:587
  525.7 3.9 copy-start.2
  527.1 2.6 collective-permute-start.3
  528.1 3.1 copy-start.6
Sparse Core Ops, SparseCore 0:
  269.7 80.0 reduce-scatter.2
  479.0 46.6 reduce-scatter.4

commit v5 on v4

--- a/solution.py
+++ b/solution.py
@@ -11,8 +11,8 @@
 NY = 4
 NZ = 4
 FIRST_ORDER = (0, 2, 3, 1, 6, 8, 4, 2, 3, 3, 2, 2, 3, 3, 3, 2, 6, 2, 2, 2, 6, 5, 5, 3, 8, 5, 5, 5, 5, 3, 2, 4, 0, 4, 0, 1, 8, 4, 0, 0, 1, 0, 1, 0, 8, 1, 0, 1, 6, 3, 3, 7, 1, 6, 1, 0, 0, 3, 3, 3, 1, 7, 7, 1, 7, 7, 0, 3, 1)
-THIRD_ORDER = (1, 2, 0, 1, 0, 1, 2, 1, 2, 0, 0, 0, 2, 1, 1, 1)
-FOURTH_ORDER = (0, 1, 2, 0, 1, 2, 2, 1, 2, 0, 2, 2, 2, 0, 1)
+THIRD_ORDER = (0, 2, 2, 0, 2, 1, 2, 2, 2, 2, 1, 1, 1, 0, 0, 2, 0, 1, 1, 1, 2, 2)
+FOURTH_ORDER = (2, 2, 2, 0, 1, 2, 2, 1, 2, 0, 2, 1, 1, 2, 1, 1, 1, 0, 0, 2, 2)
 
 
 def gelu_fwd(pre_act):
@@ -374,14 +374,103 @@
     store.wait()
 
 
-def exchange_sums(net, part, dst, tmp):
-    rows, cols = dst.shape[1:]
-
-    def piece(i, h):
-        return part.at[rows_of(0, rows, h), pl.ds(pl.multiple_of(i * cols, cols), cols)]
-
-    yield from exchange(
-        net, net.y, NY, net.at_y(1), net.at_y(-1), piece, lambda j, side, h: dst.at[side, rows_of(0, rows, h), :], tmp)
+def block_tiles(out, lhs, w, base, by_rows, wbuf, wsem):
+    size = out.shape[1] // 4
+
+    def fetch(i, slot):
+        t = pl.ds(pl.multiple_of(base + i * size, size), size)
+        return pltpu.make_async_copy(w.at[t, :] if by_rows else w.at[:, t], wbuf.at[slot], wsem.at[slot])
+
+    fetch(0, 0).start()
+
+    @pl.loop(0, 4)
+    def _(i):
+        slot = lax.rem(i, 2)
+
+        @pl.when(i < 3)
+        def _():
+            fetch(i + 1, 1 - slot).start()
+
+        fetch(i, slot).wait()
+        dims = (((1,), (1 if by_rows else 0,)), ((), ()))
+        out[:, pl.ds(pl.multiple_of(i * size, size), size)] = lax.dot_general(
+            lhs[...], wbuf[slot], dims, preferred_element_type=jnp.float32)
+
+
+def add_own(got, own, k):
+    rows = got.shape[0]
+
+    @pl.loop(0, rows, step=16)
+    def _(r):
+        here = pl.ds(pl.multiple_of(r, 16), 16)
+        got[here, :] += own[pl.ds(pl.multiple_of(k * rows + r, 16), 16), :]
+
+
+def add_all(out, own, others, order):
+    rows = out.shape[0]
+    size = out.shape[1] // len(order)
+
+    @pl.loop(0, rows, step=16)
+    def _(r):
+        here = pl.ds(pl.multiple_of(r, 16), 16)
+        total = (own[here, :] + others[0, here, :] + others[1, here, :] + others[2, here, :]).astype(out.dtype)
+        for n, b in enumerate(order):
+            out[here, b * size:(b + 1) * size] = total[:, n * size:(n + 1) * size]
+
+
+def summed(net, lhs, w, by_rows, dst, order, lv, wbuf, parts, got, others, tmp, out, sem, wsem):
+    rows, cols = got.shape[1:]
+    load = pltpu.make_async_copy(lhs, lv, sem)
+    load.start()
+    load.wait()
+    other = pl.ds(pl.multiple_of((1 - net.k) * rows, rows), rows)
+    up, down = net.at_y(1), net.at_y(-1)
+    half = rows // 2
+    lower, upper = pl.ds(0, half), pl.ds(half, half)
+    swaps = []
+
+    def part(n):
+        base = rot(net.y, (2, 1, 3, 0)[n], NY) * cols
+        block_tiles(parts.at[n], lv, w, base, by_rows, wbuf, wsem)
+        swaps.append(net.send(parts.at[n, other], got.at[n], net.partner()))
+
+    def add(n):
+        swaps[n].wait_recv()
+        add_own(got.at[n], parts.at[n], net.k)
+
+    part(0)
+    yield []
+    part(1)
+    yield [swaps[0]]
+    add(0)
+    part(2)
+    lo = net.send(got.at[0, lower], tmp.at[0], up)
+    hi = net.send(got.at[0, upper], tmp.at[1], down)
+    yield [swaps[1]]
+    add(1)
+    part(3)
+    e = net.send(got.at[1], others.at[0], up)
+    yield [swaps[2]]
+    add(2)
+    yield [swaps[3]]
+    add(3)
+    w_ = net.send(got.at[2], others.at[1], down)
+    yield [lo, hi]
+    lo.wait_recv()
+    lo = net.send(tmp.at[0], others.at[2, lower], up)
+    hi.wait_recv()
+    hi = net.send(tmp.at[1], others.at[2, upper], down)
+    yield [e, w_]
+    e.wait_recv()
+    w_.wait_recv()
+    yield [lo, hi]
+    lo.wait_recv()
+    hi.wait_recv()
+    add_all(out, got.at[3], others, order)
+    store = pltpu.make_async_copy(out, dst, sem)
+    store.start()
+    yield []
+    store.wait()
 
 
 def exchange_layers(net, part, dst, tmp):
@@ -483,23 +572,21 @@
     net.finish()
 
 
-def third_gather(d_pre, xf, ys, d_pre_l, x_l, yb, bd, bx, tx, ty, lsem, ssem, rsem):
+def third_gather(
+        d_pre, xf, act, w2f, d_pre_l, x_l, y_out, bd, bx, tx, lv, wbuf, parts, got, others, ty, out, lsem, wsem, ssem, rsem):
     net = Net(ssem, rsem)
-    run([layer_x(net, xf, x_l, bx, tx, lsem.at[1]), gather_dpre(net, d_pre, 0, d_pre_l, bd, lsem.at[0]), exchange_sums(net, ys, yb, ty)],
-        THIRD_ORDER)
+    run([layer_x(net, xf, x_l, bx, tx, lsem.at[1]), gather_dpre(net, d_pre, 0, d_pre_l, bd, lsem.at[0]),
+         summed(net, act, w2f, False, y_out, [0], lv, wbuf, parts, got, others, ty, out, lsem.at[2], wsem)], THIRD_ORDER)
     net.finish()
 
 
-def fourth_gather(d_pre, dxs, part, d_pre_l, dxb, part_b, bd, ty, tz, lsem, ssem, rsem):
+def fourth_gather(
+        d_pre, w1f, part, d_pre_l, dx_out, part_b, bd, lv, wbuf, parts, got, others, ty, out, tz, lsem, wsem, ssem, rsem):
     net = Net(ssem, rsem)
-    run([exchange_layers(net, part, part_b, tz), exchange_sums(net, dxs, dxb, ty), gather_dpre(net, d_pre, 1, d_pre_l, bd, lsem.at[0])],
-        FOURTH_ORDER)
+    order = [c * NZ + q for q in range(NZ) for c in range(2)]
+    run([exchange_layers(net, part, part_b, tz), gather_dpre(net, d_pre, 1, d_pre_l, bd, lsem.at[0]),
+         summed(net, d_pre, w1f, True, dx_out, order, lv, wbuf, parts, got, others, ty, out, lsem.at[1], wsem)], FOURTH_ORDER)
     net.finish()
-
-
-def blocks(a, order):
-    size = a.shape[1] // len(order)
-    return jnp.concatenate([a[:, b * size:(b + 1) * size] for b in order], axis=1)
 
 
 def comm(body, outs, bufs, n_local, n_remote, *args):
@@ -533,7 +620,6 @@
         hid = NY * hb
         tok = 2 * tb
         k = lax.rem(lax.axis_index("row"), 2)
-        y = lax.axis_index("col")
 
         w1f, w2f, xf, gf, pre_act, act, act_l, g_l = comm(
             first_kernel,
@@ -549,34 +635,27 @@
         dw_down_part = dot(act_l.reshape(NX * tok, fk), g_l.reshape(NX * tok, hb), ((0,), (0,)))
         dw_down = lax.psum_scatter(dw_down_part, "dep", scatter_dimension=0, tiled=True)
 
-        def core_sum(part):
-            keep = lax.dynamic_slice_in_dim(part, k * tb, tb, 0)
-            give = lax.dynamic_slice_in_dim(part, (1 - k) * tb, tb, 0)
-            return keep + lax.ppermute(give, "row", swap)
-
-        def col_sum(own, others):
-            return (lax.dynamic_slice_in_dim(own, y * hb, hb, 1) + others[0] + others[1] + others[2]).astype(bf16)
-
-        ys = core_sum(dot(act, w2f, ((1,), (0,))))
         d_pre, dw_down_part = lax.optimization_barrier((d_pre, dw_down_part))
-        d_pre_l0, x_l, yb = comm(
+        sum_bufs = [((4, tok, hb), f32), ((4, tb, hb), f32), ((3, tb, hb), f32), ((2, tb // 2, hb), f32), ((tb, hb), bf16)]
+        d_pre_l0, x_l, y_loc = comm(
             third_gather,
-            [((NX, tok, fk // 2), bf16), ((2 * NX, tb, hb), bf16), ((3, tb, hb), f32)],
-            [((tok, fk // 2), bf16), ((tb, hb), bf16), ((2, tb // 2, hb), bf16), ((2, tb // 2, hb), f32)], (2,), 64,
-            d_pre, xf, ys)
+            [((NX, tok, fk // 2), bf16), ((2 * NX, tb, hb), bf16), ((tb, hb), bf16)],
+            [((tok, fk // 2), bf16), ((tb, hb), bf16), ((2, tb // 2, hb), bf16), ((tok, fk), bf16), ((2, fk, hb // 4), bf16)] + sum_bufs,
+            (3, 2), 64,
+            d_pre, xf, act, w2f)
         x_l = x_l.reshape(NX * tok, hb)
 
         def up_part(d_pre_l):
             return dot(x_l, d_pre_l.reshape(NX * tok, fk // 2), ((0,), (0,)))
 
         part0 = up_part(d_pre_l0)
-        dxs = core_sum(dot(d_pre, w1f, ((1,), (1,))))
         part0, dw_down = lax.optimization_barrier((part0, dw_down))
-        d_pre_l1, dxb, part_b = comm(
+        d_pre_l1, dx_loc, part_b = comm(
             fourth_gather,
-            [((NX, tok, fk // 2), bf16), ((3, tb, hb), f32), ((3, 2 * hr // NZ, fk // 2), f32)],
-            [((tok, fk // 2), bf16), ((2, tb // 2, hb), f32), ((2, hr // NZ, fk // 2), f32)], (1,), 40,
-            d_pre, dxs, part0)
+            [((NX, tok, fk // 2), bf16), ((tb, hb), bf16), ((3, 2 * hr // NZ, fk // 2), f32)],
+            [((tok, fk // 2), bf16), ((tok, fk), bf16), ((2, hb // 4, fk), bf16)] + sum_bufs + [((2, hr // NZ, fk // 2), f32)],
+            (2, 2), 40,
+            d_pre, w1f, part0)
         own = lax.dynamic_slice_in_dim(part0, lax.axis_index("dep") * (2 * hr // NZ), 2 * hr // NZ, 0)
         totals = [own + part_b[0] + part_b[1] + part_b[2],
                   lax.psum_scatter(up_part(d_pre_l1), "dep", scatter_dimension=0, tiled=True)]
@@ -587,7 +666,6 @@
             take = lax.ppermute(jnp.where(k == 0, total[1], total[0]), "row", swap)
             outs.append((jnp.where(k == 0, keep, take), jnp.where(k == 0, take, keep)))
         dw_up = jnp.concatenate([outs[0][0], outs[1][0], outs[0][1], outs[1][1]], axis=1)
-        natural = [2 * q + c for c in range(2) for q in range(NZ)]
-        return col_sum(ys, yb), blocks(col_sum(dxs, dxb), natural), dw_up, dw_down
+        return y_loc, dx_loc, dw_up, dw_down
 
     return jax.shard_map(local_block, mesh=mesh, in_specs=(act_spec, wgt_spec, wgt_spec, act_spec), out_specs=(act_spec, act_spec, grad_spec, grad_spec), check_vma=False)

time: 539 us -> 518 us (0.961)
  Pallas kernels: 372 us -> 397 us
  matrix products: 76.5 us -> 51.6 us
  other arithmetic: 19.7 us -> 5.69 us
  local copies, waits for them, and re-layouts: 12.9 us -> 1.6 us
    pallas_call x3, Pallas kernels: 372 us -> 397 us  [comm(): pl.pallas_call(body, out_shape=[jax.ShapeDtypeStruct(s, d) for s, d in ou...]
    dot_general x6 -> x4, matrix products: 76.5 us -> 51.6 us  [dot(): return lax.dot_general(a, b, (dims, ((), ())), preferred_element_type=f32)]
    add x2 -> x0, other arithmetic: 10.8 us -> none  [core_sum(): return keep + lax.ppermute(give, 'row', swap)]
    dynamic_slice x2 -> x0, local copies, waits for them, and re-layouts: 7.25 us -> none  [core_sum(): give = lax.dynamic_slice_in_dim(part, (1 - k) * tb, tb, 0)]
  transfers between devices with their start and end apart: 6 -> 4, of which waited for: 2 -> 2; matrix products, arithmetic and copies ran while one was open for 14% -> 6% of each run, Pallas kernels for 12% -> 14%
where the time goes in v5:
time: 518 us; the launch traced here: 517 us
  Pallas kernels  397 us (77%)
  matrix products  51.6 us (10%)
  waiting for transfers between devices  44.7 us (9%)
  between operations  14.1 us (3%)
  other arithmetic  5.69 us (1%)
    pallas_call x3, Pallas kernels, comm(): pl.pallas_call(body, out_shape=[jax.ShapeDtypeStruct(s, d) for s, d in ou...  397 us
    dot_general x4, matrix products, dot(): return lax.dot_general(a, b, (dims, ((), ())), preferred_element_type=f32)  51.6 us
    reduce_scatter x1, waiting for transfers between devices, local_block(): lax.psum_scatter(up_part(d_pre_l1), 'dep', scatter_dimension=0, tiled=True)  43.2 us
  transfers between devices with their start and end apart: 4, of which 2 were waited for; matrix products, arithmetic and copies ran while one was open for 6% of the time, Pallas kernels for 14%

profile of v5, /device:TPU:1, one launch (start us, length us, event | category | flops | bytes accessed | tf_op | source)
XLA Modules:
  0.0 516.9 jit_solution(8951549853731577964)
XLA Ops:
  7.2 0.0 reduce-scatter.3.cloned.1.call-start
  7.2 247.8 %shard_map.75 = (bf16[4096,2048]{1,0:T(8,128)(2,1)}, bf16[2048,4096]{1,0:T(8,128)(2,1)}, bf16[512,4096]{1,0:T(8,128)(2,1)}, bf16[512,4096]{1,0:T(8,128)(2,1)}, f...) custom-call(bf16[512,4096]{1,0:T(8,128)(2,1)} %w1.1, ...), custom_call_target="tpu_custom_call" | custom-call | flops 80000000000 | bytes 67108864 | tf_op jit(solution)/shard_map/pallas_call | solution.py:594
  255.0 14.6 %fusion.7 = f32[2048,1024]{1,0:T(8,128)} fusion(bf16[2048,2048]{1,0:T(8,128)(2,1)} %bitcast.23, bf16[2048,1024]{1,0:T(8,128)(2,1)} %bitcast.26), kind=kOutput, calls=%fused_computation.21 | convolution fusion | flops 8589934592 | bytes 20971520 | tf_op jit(solution)/shard_map/dot_general | solution.py:614
  269.6 0.0 reduce-scatter.3.cloned.1.call-update
  269.6 0.2 reduce-scatter.5.cloned.1.call-start
  269.8 17.1 %fusion.6.d_pre = bf16[512,2048]{1,0:T(8,128)(2,1)} fusion(f32[512,2048]{1,0:T(8,128)} %get-tuple-element.23, bf16[512,4096]{1,0:T(8,128)(2,1)} %get-tuple-element.21, bf16[2048,4096]{1,0:T(8,128)(2,1)} %get-tuple-element.22.w2f), kind=kOutput, calls=%fused_computation.8 | convolution fusion | flops 8609857536 | bytes 27262976 | tf_op jit(solution)/shard_map/dot_general | solution.py:614
  286.9 74.5 %shard_map.76 = (bf16[4,512,1024]{2,1,0:T(8,128)(2,1)}, bf16[8,256,1024]{2,1,0:T(8,128)(2,1)}, bf16[256,1024]{1,0:T(8,128)(2,1)}) custom-call(bf16[512,2048]{1,0:T(8,128)(2,1)} %fusion.6.d_pre, bf16[512,4096]{1,0:T(8,128)(2,1)} %get-tuple-element.27.xf, bf16[512,2048]{1,0:T(8,128)(2,1)} %get-tuple-element.28.act, bf16[2048,4096]{1,0:T(8,128)(2,1)} %get-tuple-element.22.w2f), custom_call_target="tpu_custom_call" | custom-call | flops 80000000000 | bytes 67108864 | tf_op jit(solution)/shard_map/pallas_call | solution.py:594
  361.4 10.0 %fusion.8.part = f32[1024,1024]{1,0:T(8,128)} fusion(bf16[2048,1024]{1,0:T(8,128)(2,1)} %bitcast.24, bf16[2048,1024]{1,0:T(8,128)(2,1)} %bitcast.27), kind=kOutput, calls=%fused_computation.22 | convolution fusion | flops 4294967296 | bytes 12582912 | tf_op jit(solution)/shard_map/dot_general | solution.py:614
  371.4 74.7 %shard_map.77 = (bf16[4,512,1024]{2,1,0:T(8,128)(2,1)}, bf16[256,1024]{1,0:T(8,128)(2,1)}, f32[3,256,1024]{2,1,0:T(8,128)}) custom-call(bf16[512,2048]{1,0:T(8,128)(2,1)} %fusion.6.d_pre, bf16[4096,2048]{1,0:T(8,128)(2,1)} %get-tuple-element.30.w1f, f32[1024,1024]{1,0:T(8,128)} %fusion.8.part), custom_call_target="tpu_custom_call" | custom-call | flops 80000000000 | bytes 67108864 | tf_op jit(solution)/shard_map/pallas_call | solution.py:594
  446.1 10.0 %fusion.9 = f32[1024,1024]{1,0:T(8,128)} fusion(bf16[2048,1024]{1,0:T(8,128)(2,1)} %bitcast.25, bf16[2048,1024]{1,0:T(8,128)(2,1)} %bitcast.28), kind=kOutput, calls=%fused_computation.23 | convolution fusion | flops 4294967296 | bytes 12582912 | tf_op jit(solution)/shard_map/dot_general | solution.py:614
  456.1 0.0 reduce-scatter.5.cloned.1.call-update
  456.1 2.6 bitcast_add_fusion
  458.7 0.1 slice_select_fusion.2
  458.8 0.9 collective-permute-start
  459.7 43.2 %reduce-scatter.5.cloned.1.call-done = f32[256,1024]{1,0:T(8,128)} async-done(((f32[1024,1024]{1,0:T(8,128)}), f32[256,1024]{1,0:T(8,128)}) %reduce-scatter.5.cloned.1.call-update) | async-done | bytes 1048592 | tf_op jit(solution)/shard_map/reduce_scatter | solution.py:661
  503.0 1.3 slice_select_fusion
  504.3 1.0 collective-permute-start.1
  505.3 0.0 collective-permute-done
  505.3 0.1 broadcast_select_fusion.3
  505.4 1.4 collective-permute-done.1
  506.8 0.1 broadcast_select_fusion.2
  507.0 1.5 pad_maximum_fusion
  508.4 0.8 copy.10
  509.2 0.8 copy.11
  (7 shorter events, 0.0 us)
Async XLA Ops:
  7.2 364.2 %reduce-scatter.3.cloned.1.call-start = ((), (), s32[]{:S(2)}) async-start(), calls=%async_computation.2 | async-start | bytes 10485760 | tf_op jit(solution)/shard_map/reduce_scatter | solution.py:636
  269.6 233.4 %reduce-scatter.5.cloned.1.call-start = ((), (), s32[]{:S(2)}) async-start(), calls=%async_computation.3 | async-start | bytes 5242880 | tf_op jit(solution)/shard_map/reduce_scatter | solution.py:661
  458.8 46.5 %collective-permute-start = (f32[128,1024]{1,0:T(8,128)S(1)}, f32[128,1024]{1,0:T(8,128)S(1)}, u32[]{:S(2)}, u32[]{:S(2)}) collective-permute-start(f32[128,1024]{1,0:T(8,128)S(1)} %slice_select_fusion.2), channel_id=1, source_target_pairs={{0,1},{1,0},{2,3},{3,2},{4,5},{5,4},{6,7},{7,6},{8,9},{9,8},{10,11... | collective-permute-start | bytes 1572872 | tf_op jit(solution)/shard_map/ppermute | solution.py:666
  503.0 3.9 copy-start
  504.3 2.5 collective-permute-start.1
  505.3 3.1 copy-start.1
  505.4 3.8 copy-start.2
Sparse Core Ops, SparseCore 0:
  269.7 80.0 reduce-scatter.2
  456.2 46.6 reduce-scatter.4

commit v6 on v5

--- a/solution.py
+++ b/solution.py
@@ -11,8 +11,8 @@
 NY = 4
 NZ = 4
 FIRST_ORDER = (0, 2, 3, 1, 6, 8, 4, 2, 3, 3, 2, 2, 3, 3, 3, 2, 6, 2, 2, 2, 6, 5, 5, 3, 8, 5, 5, 5, 5, 3, 2, 4, 0, 4, 0, 1, 8, 4, 0, 0, 1, 0, 1, 0, 8, 1, 0, 1, 6, 3, 3, 7, 1, 6, 1, 0, 0, 3, 3, 3, 1, 7, 7, 1, 7, 7, 0, 3, 1)
-THIRD_ORDER = (0, 2, 2, 0, 2, 1, 2, 2, 2, 2, 1, 1, 1, 0, 0, 2, 0, 1, 1, 1, 2, 2)
-FOURTH_ORDER = (2, 2, 2, 0, 1, 2, 2, 1, 2, 0, 2, 1, 1, 2, 1, 1, 1, 0, 0, 2, 2)
+THIRD_ORDER = (0, 2, 0, 2, 2, 1, 2, 2, 2, 2, 1, 1, 0, 0, 0, 1, 2, 2, 2, 1, 1, 1)
+FOURTH_ORDER = (0, 2, 2, 2, 1, 0, 2, 2, 1, 2, 1, 2, 1, 1, 1, 1, 0, 2, 0, 2, 2)
 
 
 def gelu_fwd(pre_act):
@@ -353,9 +353,9 @@
         copy.wait_recv()
 
 
-def gather_dpre(net, d_pre, col, d_pre_l, buf, sem):
+def gather_dpre(net, d_pre, start, d_pre_l, buf, sem):
     rows, cols = buf.shape
-    cs = pl.ds(col * cols, cols)
+    cs = pl.ds(start, cols)
     load = pltpu.make_async_copy(d_pre.at[:, cs], buf, sem)
     load.start()
     size = rows // 4
@@ -584,7 +584,7 @@
         d_pre, w1f, part, d_pre_l, dx_out, part_b, bd, lv, wbuf, parts, got, others, ty, out, tz, lsem, wsem, ssem, rsem):
     net = Net(ssem, rsem)
     order = [c * NZ + q for q in range(NZ) for c in range(2)]
-    run([exchange_layers(net, part, part_b, tz), gather_dpre(net, d_pre, 1, d_pre_l, bd, lsem.at[0]),
+    run([exchange_layers(net, part, part_b, tz), gather_dpre(net, d_pre, d_pre.shape[1] - bd.shape[1], d_pre_l, bd, lsem.at[0]),
          summed(net, d_pre, w1f, True, dx_out, order, lv, wbuf, parts, got, others, ty, out, lsem.at[1], wsem)], FOURTH_ORDER)
     net.finish()
 
@@ -637,23 +637,25 @@
 
         d_pre, dw_down_part = lax.optimization_barrier((d_pre, dw_down_part))
         sum_bufs = [((4, tok, hb), f32), ((4, tb, hb), f32), ((3, tb, hb), f32), ((2, tb // 2, hb), f32), ((tb, hb), bf16)]
+        f0 = fk * 5 // 8
+        f1 = fk - f0
         d_pre_l0, x_l, y_loc = comm(
             third_gather,
-            [((NX, tok, fk // 2), bf16), ((2 * NX, tb, hb), bf16), ((tb, hb), bf16)],
-            [((tok, fk // 2), bf16), ((tb, hb), bf16), ((2, tb // 2, hb), bf16), ((tok, fk), bf16), ((2, fk, hb // 4), bf16)] + sum_bufs,
+            [((NX, tok, f0), bf16), ((2 * NX, tb, hb), bf16), ((tb, hb), bf16)],
+            [((tok, f0), bf16), ((tb, hb), bf16), ((2, tb // 2, hb), bf16), ((tok, fk), bf16), ((2, fk, hb // 4), bf16)] + sum_bufs,
             (3, 2), 64,
             d_pre, xf, act, w2f)
         x_l = x_l.reshape(NX * tok, hb)
 
         def up_part(d_pre_l):
-            return dot(x_l, d_pre_l.reshape(NX * tok, fk // 2), ((0,), (0,)))
+            return dot(x_l, d_pre_l.reshape(NX * tok, -1), ((0,), (0,)))
 
         part0 = up_part(d_pre_l0)
         part0, dw_down = lax.optimization_barrier((part0, dw_down))
         d_pre_l1, dx_loc, part_b = comm(
             fourth_gather,
-            [((NX, tok, fk // 2), bf16), ((tb, hb), bf16), ((3, 2 * hr // NZ, fk // 2), f32)],
-            [((tok, fk // 2), bf16), ((tok, fk), bf16), ((2, hb // 4, fk), bf16)] + sum_bufs + [((2, hr // NZ, fk // 2), f32)],
+            [((NX, tok, f1), bf16), ((tb, hb), bf16), ((3, 2 * hr // NZ, f0), f32)],
+            [((tok, f1), bf16), ((tok, fk), bf16), ((2, hb // 4, fk), bf16)] + sum_bufs + [((2, hr // NZ, f0), f32)],
             (2, 2), 40,
             d_pre, w1f, part0)
         own = lax.dynamic_slice_in_dim(part0, lax.axis_index("dep") * (2 * hr // NZ), 2 * hr // NZ, 0)
@@ -661,7 +663,7 @@
                   lax.psum_scatter(up_part(d_pre_l1), "dep", scatter_dimension=0, tiled=True)]
         outs = []
         for total in totals:
-            total = total.reshape(2, hr // NZ, fk // 2)
+            total = total.reshape(2, hr // NZ, -1)
             keep = jnp.where(k == 0, total[0], total[1])
             take = lax.ppermute(jnp.where(k == 0, total[1], total[0]), "row", swap)
             outs.append((jnp.where(k == 0, keep, take), jnp.where(k == 0, take, keep)))

time: 518 us -> 509 us (0.983)
  waiting for transfers between devices: 44.7 us -> 36.1 us
    reduce_scatter x1, waiting for transfers between devices: 43.2 us -> 34.9 us  [local_block(): lax.psum_scatter(up_part(d_pre_l1), 'dep', scatter_dimension=0, tiled=True)]
  transfers between devices with their start and end apart: 4 -> 4, of which waited for: 2 -> 2; matrix products, arithmetic and copies ran while one was open for 6% -> 6% of each run, Pallas kernels for 14% -> 15%
where the time goes in v6:
time: 509 us; the launch traced here: 508 us
  Pallas kernels  398 us (78%)
  matrix products  50.6 us (10%)
  waiting for transfers between devices  36.1 us (7%)
  between operations  14.1 us (3%)
  other arithmetic  5.83 us (1%)
    pallas_call x3, Pallas kernels, comm(): pl.pallas_call(body, out_shape=[jax.ShapeDtypeStruct(s, d) for s, d in ou...  398 us
    dot_general x4, matrix products, dot(): return lax.dot_general(a, b, (dims, ((), ())), preferred_element_type=f32)  50.6 us
    reduce_scatter x1, waiting for transfers between devices, local_block(): lax.psum_scatter(up_part(d_pre_l1), 'dep', scatter_dimension=0, tiled=True)  34.9 us
  transfers between devices with their start and end apart: 4, of which 2 were waited for; matrix products, arithmetic and copies ran while one was open for 6% of the time, Pallas kernels for 15%

profile of v6, /device:TPU:1, one launch (start us, length us, event | category | flops | bytes accessed | tf_op | source)
XLA Modules:
  0.0 508.3 jit_solution(14617039946981650569)
XLA Ops:
  7.2 0.0 reduce-scatter.3.cloned.1.call-start
  7.2 247.8 %shard_map.75 = (bf16[4096,2048]{1,0:T(8,128)(2,1)}, bf16[2048,4096]{1,0:T(8,128)(2,1)}, bf16[512,4096]{1,0:T(8,128)(2,1)}, bf16[512,4096]{1,0:T(8,128)(2,1)}, f...) custom-call(bf16[512,4096]{1,0:T(8,128)(2,1)} %w1.1, ...), custom_call_target="tpu_custom_call" | custom-call | flops 80000000000 | bytes 67108864 | tf_op jit(solution)/shard_map/pallas_call | solution.py:594
  255.0 14.7 %fusion.7 = f32[2048,1024]{1,0:T(8,128)} fusion(bf16[2048,2048]{1,0:T(8,128)(2,1)} %bitcast.23, bf16[2048,1024]{1,0:T(8,128)(2,1)} %bitcast.27), kind=kOutput, calls=%fused_computation.21 | convolution fusion | flops 8589934592 | bytes 20971520 | tf_op jit(solution)/shard_map/dot_general | solution.py:614
  269.7 0.0 reduce-scatter.3.cloned.1.call-update
  269.7 0.2 reduce-scatter.5.cloned.1.call-start
  269.9 17.1 %fusion.6.d_pre = bf16[512,2048]{1,0:T(8,128)(2,1)} fusion(f32[512,2048]{1,0:T(8,128)} %get-tuple-element.23, bf16[512,4096]{1,0:T(8,128)(2,1)} %get-tuple-element.21, bf16[2048,4096]{1,0:T(8,128)(2,1)} %get-tuple-element.22.w2f), kind=kOutput, calls=%fused_computation.8 | convolution fusion | flops 8609857536 | bytes 27262976 | tf_op jit(solution)/shard_map/dot_general | solution.py:614
  287.0 76.1 %shard_map.76 = (bf16[4,512,1280]{2,1,0:T(8,128)(2,1)}, bf16[8,256,1024]{2,1,0:T(8,128)(2,1)}, bf16[256,1024]{1,0:T(8,128)(2,1)}) custom-call(bf16[512,2048]{1,0:T(8,128)(2,1)} %fusion.6.d_pre, bf16[512,4096]{1,0:T(8,128)(2,1)} %get-tuple-element.27.xf, bf16[512,2048]{1,0:T(8,128)(2,1)} %get-tuple-element.28.act, bf16[2048,4096]{1,0:T(8,128)(2,1)} %get-tuple-element.22.w2f), custom_call_target="tpu_custom_call" | custom-call | flops 80000000000 | bytes 67108864 | tf_op jit(solution)/shard_map/pallas_call | solution.py:594
  363.1 10.5 %fusion.8.part = f32[1024,1280]{1,0:T(8,128)} fusion(bf16[2048,1024]{1,0:T(8,128)(2,1)} %bitcast.25, bf16[2048,1280]{1,0:T(8,128)(2,1)} %bitcast.24), kind=kOutput, calls=%fused_computation.22 | convolution fusion | flops 5368709120 | bytes 14680064 | tf_op jit(solution)/shard_map/dot_general | solution.py:614
  373.6 73.9 %shard_map.77 = (bf16[4,512,768]{2,1,0:T(8,128)(2,1)}, bf16[256,1024]{1,0:T(8,128)(2,1)}, f32[3,256,1280]{2,1,0:T(8,128)}) custom-call(bf16[512,2048]{1,0:T(8,128)(2,1)} %fusion.6.d_pre, bf16[4096,2048]{1,0:T(8,128)(2,1)} %get-tuple-element.30.w1f, f32[1024,1280]{1,0:T(8,128)} %fusion.8.part), custom_call_target="tpu_custom_call" | custom-call | flops 80000000000 | bytes 67108864 | tf_op jit(solution)/shard_map/pallas_call | solution.py:594
  447.5 8.3 %fusion.9 = f32[1024,768]{1,0:T(8,128)} fusion(bf16[2048,1024]{1,0:T(8,128)(2,1)} %bitcast.26, bf16[2048,768]{1,0:T(8,128)(2,1)} %bitcast.28), kind=kOutput, calls=%fused_computation.23 | convolution fusion | flops 3221225472 | bytes 10485760 | tf_op jit(solution)/shard_map/dot_general | solution.py:614
  455.9 0.0 reduce-scatter.5.cloned.1.call-update
  455.9 2.8 bitcast_add_fusion
  458.7 0.1 slice_select_fusion
  458.8 1.0 collective-permute-start
  459.8 34.9 %reduce-scatter.5.cloned.1.call-done = f32[256,768]{1,0:T(8,128)} async-done(((f32[1024,768]{1,0:T(8,128)}), f32[256,768]{1,0:T(8,128)}) %reduce-scatter.5.cloned.1.call-update) | async-done | bytes 786448 | tf_op jit(solution)/shard_map/reduce_scatter | solution.py:663
  494.7 1.2 slice_select_fusion.2
  495.9 1.0 collective-permute-start.1
  496.9 0.0 collective-permute-done
  496.9 0.1 broadcast_select_fusion.1
  497.1 1.2 collective-permute-done.1
  498.3 0.1 broadcast_select_fusion.3
  498.3 1.5 pad_maximum_fusion
  499.9 0.8 copy.10
  500.7 0.8 copy.11
  (7 shorter events, 0.0 us)
Async XLA Ops:
  7.2 366.5 %reduce-scatter.3.cloned.1.call-start = ((), (), s32[]{:S(2)}) async-start(), calls=%async_computation.2 | async-start | bytes 10485760 | tf_op jit(solution)/shard_map/reduce_scatter | solution.py:636
  269.7 225.0 %reduce-scatter.5.cloned.1.call-start = ((), (), s32[]{:S(2)}) async-start(), calls=%async_computation.3 | async-start | bytes 3932160 | tf_op jit(solution)/shard_map/reduce_scatter | solution.py:663
  458.8 38.1 %collective-permute-start = (f32[128,1280]{1,0:T(8,128)S(1)}, f32[128,1280]{1,0:T(8,128)S(1)}, u32[]{:S(2)}, u32[]{:S(2)}) collective-permute-start(f32[128,1280]{1,0:T(8,128)S(1)} %slice_select_fusion), channel_id=1, source_target_pairs={{0,1},{1,0},{2,3},{3,2},{4,5},{5,4},{6,7},{7,6},{8,9},{9,8},{10,11... | collective-permute-start | bytes 1966088 | tf_op jit(solution)/shard_map/ppermute | solution.py:668
  494.7 3.6 copy-start
  495.9 4.0 copy-start.1
  495.9 2.4 collective-permute-start.1
  497.0 3.6 copy-start.2
Sparse Core Ops, SparseCore 0:
  269.8 80.0 reduce-scatter.2
  456.0 38.5 reduce-scatter.4
